TPU v7x, 32 devices: a whole 2x2x4 slice. The times are simulated.
32 devices in a mesh: member: 4 (over y, core), lat: 8 (over z, x).
Axes of the slice: x: 2, y: 2, z: 4, core: 2. Of those that a mesh axis runs over, the one named last changes fastest.
Arguments:
- ensemble: float32 [640, 32, 256], P('member', 'lat'), may hold values from -6 to 6
- obs_cell: int32 [32, 128], P(('member', 'lat')), may hold values from 0 to 255
- obs_value: float32 [32, 128], P(('member', 'lat')), may hold values from -8 to 8
- obs_var: float32 [32, 128], P(('member', 'lat')), may hold values from 0.5 to 8
- patch_rows: int32 [32, 2], P(('member', 'lat')), may hold values from 1 to 24, 32 in all within a row
Outputs:
- analysis: float32 [640, 32, 256], P('member', 'lat')
Inputs may be any that keep to these rules, and one draw needn't show every extreme that they name: `patch_rows`: each server's 2 patch lengths sum to 32.
All inputs are finite; a program needn't handle non-finite values. Where the computation divides by a largest or mean magnitude, that divisor is 1e-20 or more.
Results may differ from a plain program's by a relative error of at most 0.0003.
Values sent between devices are 32-bit elements; how exact they have to be, the bound alone decides.
A program may use at most 64 MiB of HBM per device.

v0:
```python
import jax
import jax.numpy as jnp
from jax import lax
from jax.sharding import PartitionSpec as P

STEPS = 4


lat_coeff = 0.4
lon_coeff = 0.05
advect_coeff = 0.1


def with_halo(value, sides, width, wrap):
    for axis, dim in sides:
        size, length = (lax.axis_size(axis), value.shape[dim])
        up = [(i, (i + 1) % size) for i in range(size if wrap else size - 1)]
        down = [(j, i) for i, j in up]
        last = lax.slice_in_dim(value, length - width, length, axis=dim)
        initial = lax.slice_in_dim(value, 0, width, axis=dim)
        before = lax.ppermute(last, axis, up)
        after = lax.ppermute(initial, axis, down)
        value = jnp.concatenate([before, value, after], axis=dim)
    return value


def advance(padded):
    centre = padded[:, 1:-1]
    northern = padded[:, :-2]
    southern = padded[:, 2:]
    eastern = jnp.roll(centre, -1, axis=2)
    western = jnp.roll(centre, 1, axis=2)
    return (
        centre
        + lat_coeff * (northern + southern - 2.0 * centre)
        + lon_coeff * (eastern + western - 2.0 * centre)
        - advect_coeff * centre * (eastern - western)
    )


def observe(states, cell_index, values):
    observed = jnp.take(states, cell_index, axis=1)
    obs_mean = jnp.mean(observed, axis=0)
    return (observed - obs_mean, values - obs_mean)


def localize(obs_rows, rel_cols, first_row, row_count, lat_scale, width_cols):
    lower = first_row.astype(jnp.float32)
    upper = lower + row_count.astype(jnp.float32) - 1.0
    lat_gap = jnp.maximum(jnp.maximum(lower - obs_rows, obs_rows - upper), 0.0) / lat_scale
    lon_gap = jnp.maximum(jnp.maximum(-rel_cols, rel_cols - (width_cols - 1.0)), 0.0) / width_cols
    return jnp.exp(-lat_gap * lat_gap - lon_gap * lon_gap)


def dot3(left, right):
    return jnp.matmul(left, right, precision=lax.Precision.HIGH, preferred_element_type=jnp.float32)


def analyse(states, spread, obs_meta, lengths, width_cols):
    members = states.shape[0]
    cell_total = states.shape[1]
    lat_total = cell_total // width_cols
    near = spread.shape[1]
    state_mean = jnp.mean(states, axis=0)
    anomaly = states - state_mean
    starts = jnp.cumsum(lengths) - lengths
    cell_rows = jnp.arange(cell_total, dtype=jnp.int32) // width_cols
    identity = jnp.eye(members, dtype=jnp.float32)
    products = dot3(spread.T, jnp.concatenate([spread, anomaly], axis=1))
    common, crossed = products[:, :near], products[:, near:]
    innov = obs_meta[0]
    shrink = jnp.zeros((cell_total,), jnp.float32)
    shift = state_mean
    weights_all = jnp.zeros((near, cell_total), jnp.float32)
    for patch in range(lengths.shape[0]):
        weights = (
            localize(
                obs_meta[2],
                obs_meta[3],
                starts[patch],
                lengths[patch],
                lat_total / 4.0,
                float(width_cols),
            )
            / obs_meta[1]
        )
        scale = jnp.sqrt(weights)
        gram_matrix = (members - 1.0) * identity + jnp.dot(
            spread * weights, spread.T, preferred_element_type=jnp.float32
        )
        bound = jnp.max(jnp.sum(jnp.abs(gram_matrix), axis=1))
        alpha = (members - 1.0) / bound
        x = common * scale[:, None] * (scale / bound)[None, :]
        c0 = 2.25 + alpha * (-2.4375 + alpha * (1.6875 + alpha * (-0.5625 + alpha * 0.0625)))
        c1 = -2.4375 + alpha * (3.375 + alpha * (-1.6875 + alpha * 0.25))
        c2 = 1.6875 + alpha * (-1.6875 + alpha * 0.375)
        c3 = -0.5625 + alpha * 0.25
        c4 = 0.0625
        x2 = dot3(x, x)
        x34 = dot3(x2, jnp.concatenate([x, x2], axis=1))
        x3, x4 = x34[:, :near], x34[:, near:]
        low = c2 * x + c3 * x2 + c4 * x3
        high = c1 * x + c2 * x2 + c3 * x3 + c4 * x4
        block = jnp.concatenate([crossed * scale[:, None], (scale * innov)[:, None]], axis=1)
        both = dot3(jnp.concatenate([low, high], axis=0), block)
        b1 = c1 * block + both[:near]
        b2 = c0 * block + both[near:]
        b3 = c0 * b2 + dot3(high, b2)
        mixed = alpha * c0 * b1 + b3
        got = 1.5 * b1 - 0.5 * (
            alpha * c0 * c0 * b1
            + c0 * mixed
            + dot3(high, mixed)
            + alpha * (c1 * b3 + dot3(low, b3))
        )
        base = c0 * (1.5 - 0.5 * alpha * c0 * c0)
        driven = base * block[:, -1] + jnp.sum(x * got[:, -1][None, :], axis=1)
        again = jnp.sum(x * driven[None, :], axis=1)
        mean_part = (
            jnp.sum(block[:, :-1] * (base * driven)[:, None] + got[:, :-1] * again[:, None], axis=0)
            / bound
        )
        cell_mask = (cell_rows >= starts[patch]) & (cell_rows < starts[patch] + lengths[patch])
        root_scale = jnp.sqrt((members - 1.0) / bound)
        shift = shift + jnp.where(cell_mask, mean_part, 0.0)
        shrink = jnp.where(cell_mask, root_scale * base, shrink)
        weights_all = jnp.where(
            cell_mask[None, :], got[:, :-1] * (scale * (root_scale / bound))[:, None], weights_all
        )
    return shift + shrink * anomaly + dot3(spread, weights_all)


def per_device(ensemble, obs_cell, obs_value, obs_var, patch_rows):
    fields = ensemble
    members_dev = fields.shape[0]
    lat_rows = fields.shape[1]
    lon_cells = fields.shape[2]
    lat_count = lax.axis_size("lat")
    member_count = lax.axis_size("member")
    servers = lat_count * member_count
    width_cols = lon_cells // servers
    padded = with_halo(fields, (("lat", 1),), STEPS, False)
    global_rows = (
        lax.axis_index("lat") * lat_rows + jnp.arange(lat_rows + 2 * STEPS, dtype=jnp.int32) - STEPS
    )
    inside = ((global_rows >= 0) & (global_rows < lat_rows * lat_count)).astype(jnp.float32)
    for step_index in range(STEPS):
        padded = advance(padded)
        keeper = inside[step_index + 1 : inside.shape[0] - step_index - 1]
        padded = padded * keeper[None, :, None]
    fields = padded
    blocks = fields.reshape(1, members_dev, lat_rows, lon_cells)
    received = lax.all_to_all(blocks, ("member", "lat"), split_axis=3, concat_axis=0, tiled=True)
    strip = received.reshape(member_count, lat_count, members_dev, lat_rows, width_cols)
    strip = strip.transpose(0, 2, 1, 3, 4).reshape(
        member_count * members_dev, lat_count * lat_rows, width_cols
    )
    members = strip.shape[0]
    lat_total = strip.shape[1]
    states = strip.reshape(members, lat_total * width_cols)
    cell_index = obs_cell[0]
    obs_count = cell_index.shape[0]
    spread, innov = observe(states, cell_index, obs_value[0])
    obs_meta = jnp.stack(
        [
            innov,
            obs_var[0],
            (cell_index // width_cols).astype(jnp.float32),
            (cell_index % width_cols).astype(jnp.float32),
        ]
    )
    near_spread, near_meta = (
        with_halo(spread, ((("member", "lat"), 1),), obs_count, True),
        with_halo(obs_meta, ((("member", "lat"), 1),), obs_count, True),
    )
    shifts = jnp.repeat(jnp.array([-1.0, 0.0, 1.0], jnp.float32), obs_count) * width_cols
    near_meta = jnp.concatenate([near_meta[:3], (near_meta[3] + shifts)[None, :]], axis=0)
    analysed = analyse(states, near_spread, near_meta, patch_rows[0], width_cols)
    analysed = analysed.reshape(members, lat_total, width_cols)
    outgoing = analysed.reshape(member_count, members_dev, lat_count, lat_rows, width_cols)
    outgoing = outgoing.transpose(0, 2, 1, 3, 4).reshape(servers, members_dev, lat_rows, width_cols)
    returned = lax.all_to_all(outgoing, ("member", "lat"), split_axis=0, concat_axis=3, tiled=True)
    return returned.reshape(members_dev, lat_rows, lon_cells)


def solution(mesh):
    in_specs = (
        P("member", "lat", None),
        P(("member", "lat"), None),
        P(("member", "lat"), None),
        P(("member", "lat"), None),
        P(("member", "lat"), None),
    )
    out_specs = P("member", "lat", None)
    return jax.shard_map(
        per_device, mesh=mesh, in_specs=in_specs, out_specs=out_specs, check_vma=False
    )
```

profile of v0, /device:TPU:0, one launch (start us, length us, event | category | flops | bytes accessed | tf_op | source)
XLA Modules:
  0.0 164.4 jit_solution(16774635268156717155)
XLA Ops:
  0.0 1.3 copy.83
  1.3 4.9 %collective-permute-start = (f32[160,4,256]{2,0,1:T(8,128)S(1)}, f32[160,4,256]{2,0,1:T(8,128)S(1)}, u32[]{:S(2)}, u32[]{:S(2)}) collective-permute-start(f32[160,4,256]{2,0,1:T(8,128)S(1)} %copy.83), channel_id=1, source_target_pairs={{0,1},{1,2},{2,3},{3,4},{4,5},{5,6},{6,7},{8,9},{9,10},{10,11},{11... | collective-permute-start | bytes 1966088 | tf_op jit(solution)/shard_map/ppermute | solution.py:21
  6.2 1.3 collective-permute-start.1
  7.8 0.8 reduce-window.9
  8.6 25.5 %collective-permute-done = f32[160,4,256]{2,0,1:T(8,128)S(1)} collective-permute-done((f32[160,4,256]{2,0,1:T(8,128)S(1)}, f32[160,4,256]{2,0,1:T(8,128)S(1)}, u32[]{:S(2)}, u32[]{:S(2)}) %collective-permute-start) | collective-permute-done | bytes 655392 | tf_op jit(solution)/shard_map/ppermute | solution.py:21
  35.3 1.1 fusion.9
  37.0 0.9 fusion.25
  40.1 1.3 copy.86
  41.4 6.6 %all-to-all-start = ((f32[1,160,4,256]{1,2,0,3:T(4,128)}), f32[1,160,4,256]{1,2,0,3:T(4,128)S(1)}, u32[]{:S(2)}, u32[]{:S(2)}) async-start(f32[1,160,4,256]{1,2,0,3:T(4,128)} %copy.86), calls=%async_computation | async-start | bytes 2097152 | tf_op jit(solution)/shard_map/all_to_all | solution.py:153
  54.3 21.2 %all-to-all-done = f32[1,160,4,256]{1,2,0,3:T(4,128)S(1)} async-done(((f32[1,160,4,256]{1,2,0,3:T(4,128)}), f32[1,160,4,256]{1,2,0,3:T(4,128)S(1)}, u32[]{:S(2)}, u32[]{:S(2)}) %all-to-all-start) | async-done | bytes 655392 | tf_op jit(solution)/shard_map/all_to_all | solution.py:153
  77.0 0.8 gather_fusion
  78.2 0.8 collective-permute-start.4
  79.0 4.6 %collective-permute-start.5 = (f32[4,128]{1,0:T(4,128)S(1)}, f32[4,128]{1,0:T(4,128)S(1)}, u32[]{:S(2)}, u32[]{:S(2)}) collective-permute-start(f32[4,128]{1,0:T(4,128)S(1)} %pad_maximum_fusion.22), channel_id=1, source_target_pairs={{1,0},{2,1},{3,2},{4,3},{5,4},{6,5},{7,6},{8,7},{9,8},{10,9},{11,1... | collective-permute-start | bytes 6152 | tf_op jit(solution)/shard_map/ppermute | solution.py:22
  83.7 5.3 %collective-permute-start.3 = (f32[640,128]{1,0:T(8,128)S(1)}, f32[640,128]{1,0:T(8,128)}, u32[]{:S(2)}, u32[]{:S(2)}) collective-permute-start(f32[640,128]{1,0:T(8,128)S(1)} %subtract_bitcast_fusion), channel_id=1, source_target_pairs={{1,0},{2,1},{3,2},{4,3},{5,4},{6,5},{7,6},{8,7},{9,8},{10,9},{11,1... | collective-permute-start | bytes 983048 | tf_op jit(solution)/shard_map/ppermute | solution.py:22
  90.4 6.6 %collective-permute-done.2 = f32[640,128]{1,0:T(8,128)S(1)} collective-permute-done((f32[640,128]{1,0:T(8,128)S(1)}, f32[640,128]{1,0:T(8,128)S(1)}, u32[]{:S(2)}, u32[]{:S(2)}) %collective-permute-start.2) | collective-permute-done | bytes 327712 | tf_op jit(solution)/shard_map/ppermute | solution.py:21
  97.0 2.5 %collective-permute-done.3 = f32[640,128]{1,0:T(8,128)} collective-permute-done((f32[640,128]{1,0:T(8,128)S(1)}, f32[640,128]{1,0:T(8,128)}, u32[]{:S(2)}, u32[]{:S(2)}) %collective-permute-start.3) | collective-permute-done | bytes 327712 | tf_op jit(solution)/shard_map/ppermute | solution.py:22
  99.5 1.8 %fusion.3 = f32[640]{0:T(1024)S(1)} fusion(f32[640,128]{1,0:T(8,128)} %collective-permute-done.3, f32[640,128]{1,0:T(8,128)S(1)} %subtract_bitcast_fusion, f32[640,128]{1,0:T(8,128)S(1)} %collective-permute-done.2, f32[384]{0:T(512)S(1)} %get-tuple-element.25), kind=kOutput, calls=%fused_computation.6 | convolution fusion | flops 317848960 | bytes 987136 | tf_op jit(solution)/shard_map/dot_general | solution.py:88
  102.7 1.8 %fusion.1 = f32[640]{0:T(1024)S(1)} fusion(f32[640,128]{1,0:T(8,128)} %collective-permute-done.3, f32[640,128]{1,0:T(8,128)S(1)} %subtract_bitcast_fusion, f32[640,128]{1,0:T(8,128)S(1)} %collective-permute-done.2, f32[384]{0:T(512)S(1)} %get-tuple-element.53), kind=kOutput, calls=%fused_computation.4 | convolution fusion | flops 317848960 | bytes 987136 | tf_op jit(solution)/shard_map/dot_general | solution.py:88
  109.3 2.6 %fusion.10 = f32[384,640]{1,0:T(8,128)S(1)} fusion(f32[640,256]{1,0:T(8,128)S(1)} %broadcast_subtract_fusion, f32[640,128]{1,0:T(8,128)} %collective-permute-done.3, f32[640,128]{1,0:T(8,128)S(1)} %subtract_bitcast_fusion, f32[640,128]{1,0:T(8,128)S(1)} %collective-permute-done.2), kind=kOutput, calls=%fused_computation.16 | convolution fusion | flops 945438720 | bytes 2621440 | tf_op jit(solution)/shard_map/dot_general | solution.py:56
  113.0 0.8 copy-done
  113.9 2.1 %fusion.34 = f32[384,768]{1,0:T(8,128)} fusion(f32[384,384]{1,0:T(8,128)S(1)} %fusion.136, f32[384,384]{1,0:T(8,128)S(1)} %get-tuple-element.47), kind=kOutput, calls=%fused_computation.51 | convolution fusion | flops 679772160 | bytes 2359296 | tf_op jit(solution)/shard_map/dot_general | solution.py:56
  116.7 1.1 fusion.42
  118.4 1.3 fusion.46
  119.6 0.8 convolution_add_fusion.3
  121.2 1.0 fusion.32
  122.1 0.8 copy-done.3
  123.2 1.5 fusion.38
  126.3 0.9 fusion.28
  128.4 2.4 %fusion.104 = (f32[256]{0:T(256)S(1)}, pred[256]{0:T(512)(128)(4,1)S(1)}, pred[256]{0:T(512)(128)(4,1)S(1)}) fusion(f32[256]{0:T(256)S(1)} %add_reduce_fusion, f32[256]{0:T(256)S(1)} %copy-done.17, f32[256]{0:T(256)S(1)} %add_reduce_fusion.1, f32[]{:T(128)} %reduce_max.19, f32[]{:T(128)} %reduce_max.18, s32[]{:T(128)S(6)} %add.404, s32[]{:T(128)} %bitcast.8, ...), kind=kLoop, calls=%fused_computation.203 | loop fusion | flops 5120 | bytes 4632 | tf_op jit(solution)/shard_map/add | solution.py:125
  130.9 1.8 %convolution_add_fusion = f32[640,256]{1,0:T(8,128)S(1)} fusion(f32[640,256]{1,0:T(8,128)S(1)} %copy-done.7, f32[640,128]{1,0:T(8,128)} %collective-permute-done.3, f32[640,128]{1,0:T(8,128)S(1)} %copy-done.9, f32[640,128]{1,0:T(8,128)S(1)} %copy-done.11, f32[384,257]{1,0:T(8,128)S(1)} %copy-done.4, f32[384,257]{1,0:T(8,128)S(1)} %fusion.28, ...), kind=kOutput, calls=%fused_computation.36 | convolution fusion | flops 378863616 | bytes 3087360 | tf_op jit(solution)/shard_map/dot_general | solution.py:56
  133.9 29.2 %all_to_all.30 = f32[32,160,4,8]{1,3,2,0:T(8,128)S(1)} all-to-all(f32[32,160,4,8]{1,3,2,0:T(8,128)S(1)} %bitcast.110), channel_id=1, replica_groups=mesh['member'=4,'lat'=8] {'member','lat'}, dimensions={0} | all-to-all | bytes 1310720 | tf_op jit(solution)/shard_map/all_to_all | solution.py:182
  163.2 1.1 copy.107
  (128 shorter events, 19.1 us)
Async XLA Ops:
  0.0 34.2 %copy-start.5 = (f32[160,4,256]{2,1,0:T(4,128)S(1)}, f32[160,4,256]{2,1,0:T(4,128)}, u32[]{:S(2)}) copy-start(f32[160,4,256]{2,1,0:T(4,128)} %param.6) | copy-start | bytes 1966084
  1.3 32.9 %collective-permute-start = (f32[160,4,256]{2,0,1:T(8,128)S(1)}, f32[160,4,256]{2,0,1:T(8,128)S(1)}, u32[]{:S(2)}, u32[]{:S(2)}) collective-permute-start(f32[160,4,256]{2,0,1:T(8,128)S(1)} %copy.83), channel_id=1, source_target_pairs={{0,1},{1,2},{2,3},{3,4},{4,5},{5,6},{6,7},{8,9},{9,10},{10,11},{11... | collective-permute-start | bytes 1966088 | tf_op jit(solution)/shard_map/ppermute | solution.py:21
  6.2 28.2 %collective-permute-start.1 = (f32[160,4,256]{2,0,1:T(8,128)S(1)}, f32[160,4,256]{2,0,1:T(8,128)S(1)}, u32[]{:S(2)}, u32[]{:S(2)}) collective-permute-start(f32[160,4,256]{2,0,1:T(8,128)S(1)} %copy.83), channel_id=1, source_target_pairs={{1,0},{2,1},{3,2},{4,3},{5,4},{6,5},{7,6},{9,8},{10,9},{11,10},{12... | collective-permute-start | bytes 1966088 | tf_op jit(solution)/shard_map/ppermute | solution.py:22
  40.0 8.0 %copy-start.21 = (s32[1,2]{1,0:T(1,128)S(1)}, s32[1,2]{1,0:T(1,128)}, u32[]{:S(2)}) copy-start(s32[1,2]{1,0:T(1,128)} %param.10) | copy-start | bytes 28
  40.0 14.1 %copy-start.23 = (s32[1,128]{1,0:T(1,128)S(1)}, s32[1,128]{1,0:T(1,128)}, u32[]{:S(2)}) copy-start(s32[1,128]{1,0:T(1,128)} %param.7) | copy-start | bytes 1540
  40.1 14.1 %copy-start.20 = (f32[3]{0:T(128)S(1)}, f32[3]{0:T(128)}, u32[]{:S(2)}) copy-start(f32[3]{0:T(128)} %constant.157) | copy-start | bytes 40
  41.4 34.1 %all-to-all-start = ((f32[1,160,4,256]{1,2,0,3:T(4,128)}), f32[1,160,4,256]{1,2,0,3:T(4,128)S(1)}, u32[]{:S(2)}, u32[]{:S(2)}) async-start(f32[1,160,4,256]{1,2,0,3:T(4,128)} %copy.86), calls=%async_computation | async-start | bytes 2097152 | tf_op jit(solution)/shard_map/all_to_all | solution.py:153
  77.0 1.1 copy-start.24
  77.0 1.1 copy-start.22
  78.2 11.6 %collective-permute-start.4 = (f32[4,128]{1,0:T(4,128)S(1)}, f32[4,128]{1,0:T(4,128)S(1)}, u32[]{:S(2)}, u32[]{:S(2)}) collective-permute-start(f32[4,128]{1,0:T(4,128)S(1)} %pad_maximum_fusion.22), channel_id=1, source_target_pairs={{0,1},{1,2},{2,3},{3,4},{4,5},{5,6},{6,7},{7,8},{8,9},{9,10},{10,1... | collective-permute-start | bytes 6152 | tf_op jit(solution)/shard_map/ppermute | solution.py:21
  79.0 10.7 %collective-permute-start.5 = (f32[4,128]{1,0:T(4,128)S(1)}, f32[4,128]{1,0:T(4,128)S(1)}, u32[]{:S(2)}, u32[]{:S(2)}) collective-permute-start(f32[4,128]{1,0:T(4,128)S(1)} %pad_maximum_fusion.22), channel_id=1, source_target_pairs={{1,0},{2,1},{3,2},{4,3},{5,4},{6,5},{7,6},{8,7},{9,8},{10,9},{11,1... | collective-permute-start | bytes 6152 | tf_op jit(solution)/shard_map/ppermute | solution.py:22
  83.6 25.7 %copy-start.8 = (f32[640,128]{1,0:T(8,128)}, f32[640,128]{1,0:T(8,128)S(1)}, u32[]{:S(2)}) copy-start(f32[640,128]{1,0:T(8,128)S(1)} %subtract_bitcast_fusion) | copy-start | bytes 983044
  83.6 13.4 %collective-permute-start.2 = (f32[640,128]{1,0:T(8,128)S(1)}, f32[640,128]{1,0:T(8,128)S(1)}, u32[]{:S(2)}, u32[]{:S(2)}) collective-permute-start(f32[640,128]{1,0:T(8,128)S(1)} %subtract_bitcast_fusion), channel_id=1, source_target_pairs={{0,1},{1,2},{2,3},{3,4},{4,5},{5,6},{6,7},{7,8},{8,9},{9,10},{10,1... | collective-permute-start | bytes 983048 | tf_op jit(solution)/shard_map/ppermute | solution.py:21
  83.7 15.8 %collective-permute-start.3 = (f32[640,128]{1,0:T(8,128)S(1)}, f32[640,128]{1,0:T(8,128)}, u32[]{:S(2)}, u32[]{:S(2)}) collective-permute-start(f32[640,128]{1,0:T(8,128)S(1)} %subtract_bitcast_fusion), channel_id=1, source_target_pairs={{1,0},{2,1},{3,2},{4,3},{5,4},{6,5},{7,6},{8,7},{9,8},{10,9},{11,1... | collective-permute-start | bytes 983048 | tf_op jit(solution)/shard_map/ppermute | solution.py:22
  89.6 0.6 copy-start.16
  89.7 19.6 %copy-start.6 = (f32[640,256]{1,0:T(8,128)}, f32[640,256]{1,0:T(8,128)S(1)}, u32[]{:S(2)}) copy-start(f32[640,256]{1,0:T(8,128)S(1)} %broadcast_subtract_fusion) | copy-start | bytes 1966084
  89.8 18.1 %copy-start.12 = (f32[1,384]{1,0:T(1,128)}, f32[1,384]{1,0:T(1,128)S(1)}, u32[]{:S(2)}) copy-start(f32[1,384]{1,0:T(1,128)S(1)} %get-tuple-element.54) | copy-start | bytes 4612
  90.4 16.8 %copy-start.14 = (f32[1,384]{1,0:T(1,128)}, f32[1,384]{1,0:T(1,128)S(1)}, u32[]{:S(2)}) copy-start(f32[1,384]{1,0:T(1,128)S(1)} %get-tuple-element.26) | copy-start | bytes 4612
  97.0 12.3 %copy-start.10 = (f32[640,128]{1,0:T(8,128)}, f32[640,128]{1,0:T(8,128)S(1)}, u32[]{:S(2)}) copy-start(f32[640,128]{1,0:T(8,128)S(1)} %collective-permute-done.2) | copy-start | bytes 983044
  113.0 0.8 copy-start
  116.0 1.9 %copy-start.1 = (f32[384,384]{1,0:T(8,128)S(1)}, f32[384,384]{1,0:T(8,128)}, u32[]{:S(2)}) copy-start(f32[384,384]{1,0:T(8,128)} %copy-done) | copy-start | bytes 1769476
  116.0 1.9 %copy-start.2 = (f32[384,768]{1,0:T(8,128)S(1)}, f32[384,768]{1,0:T(8,128)}, u32[]{:S(2)}) copy-start(f32[384,768]{1,0:T(8,128)} %fusion.34) | copy-start | bytes 3538948
  122.1 0.8 copy-start.3
  126.2 1.3 copy-start.13
  126.2 1.3 copy-start.15
  127.2 1.1 copy-start.4
  127.3 1.1 copy-start.17
  127.4 3.5 %copy-start.7 = (f32[640,256]{1,0:T(8,128)S(1)}, f32[640,256]{1,0:T(8,128)}, u32[]{:S(2)}) copy-start(f32[640,256]{1,0:T(8,128)} %copy-done.6) | copy-start | bytes 1966084
  127.4 3.5 %copy-start.9 = (f32[640,128]{1,0:T(8,128)S(1)}, f32[640,128]{1,0:T(8,128)}, u32[]{:S(2)}) copy-start(f32[640,128]{1,0:T(8,128)} %copy-done.8) | copy-start | bytes 983044
  127.4 3.5 %copy-start.11 = (f32[640,128]{1,0:T(8,128)S(1)}, f32[640,128]{1,0:T(8,128)}, u32[]{:S(2)}) copy-start(f32[640,128]{1,0:T(8,128)} %copy-done.10) | copy-start | bytes 983044
  127.4 3.5 %copy-start.18 = (f32[384]{0:T(512)S(1)}, f32[384]{0:T(512)}, u32[]{:S(2)}) copy-start(f32[384]{0:T(512)} %get-tuple-element.12) | copy-start | bytes 4612
  127.4 3.5 %copy-start.19 = (f32[384]{0:T(512)S(1)}, f32[384]{0:T(512)}, u32[]{:S(2)}) copy-start(f32[384]{0:T(512)} %get-tuple-element.56) | copy-start | bytes 4612
where the time goes:
time: 165 us; the launch traced here: 164 us
  waiting for transfers between devices  55.9 us (34%)
  blocking collectives  29.2 us (18%)
  starting transfers between devices  23.6 us (14%)
  matrix products  20.3 us (12%)
  local copies, waits for them, and re-layouts  14.7 us (9%)
  other arithmetic  12.1 us (7%)
  between operations  8.58 us (5%)
    ppermute x3, waiting for transfers between devices, with_halo(): before = lax.ppermute(last, axis, up)  32.1 us
    all_to_all x1, blocking collectives, per_device(): lax.all_to_all(outgoing, ('member', 'lat'), split_axis=0, concat_axis=3,...  29.2 us
    all_to_all x1, waiting for transfers between devices, per_device(): lax.all_to_all(blocks, ('member', 'lat'), split_axis=3, concat_axis=0, ti...  21.2 us
    dot_general x14, matrix products, dot3(): jnp.matmul(left, right, precision=lax.Precision.HIGH, preferred_element_t...  16.7 us
    ppermute x3, starting transfers between devices, with_halo(): after = lax.ppermute(initial, axis, down)  11.2 us
    all_to_all x1, starting transfers between devices, per_device(): lax.all_to_all(blocks, ('member', 'lat'), split_axis=3, concat_axis=0, ti...  6.62 us
    ppermute x3, starting transfers between devices, with_halo(): before = lax.ppermute(last, axis, up)  5.8 us
    unnamed x54, local copies, waits for them, and re-layouts  3.6 us
  transfers between devices with their start and end apart: 7, of which 4 were waited for; matrix products, arithmetic and copies ran while one was open for 2% of the time, Pallas kernels for 0%

commit v1 on v0

v1 whole, which is shorter than its diff:
```python
import functools

import jax
import jax.numpy as jnp
from jax import lax
from jax.experimental import pallas as pl
from jax.experimental.pallas import tpu as pltpu
from jax.sharding import PartitionSpec as P

STEPS = 4

lat_coeff = 0.4
lon_coeff = 0.05
advect_coeff = 0.1

MESH = pl.DeviceIdType.MESH
LANES = 128


def with_halo(value, sides, width, wrap):
    for axis, dim in sides:
        size, length = (lax.axis_size(axis), value.shape[dim])
        up = [(i, (i + 1) % size) for i in range(size if wrap else size - 1)]
        down = [(j, i) for i, j in up]
        last = lax.slice_in_dim(value, length - width, length, axis=dim)
        initial = lax.slice_in_dim(value, 0, width, axis=dim)
        before = lax.ppermute(last, axis, up)
        after = lax.ppermute(initial, axis, down)
        value = jnp.concatenate([before, value, after], axis=dim)
    return value


def advance(padded):
    centre = padded[:, 1:-1]
    northern = padded[:, :-2]
    southern = padded[:, 2:]
    eastern = jnp.roll(centre, -1, axis=2)
    western = jnp.roll(centre, 1, axis=2)
    return (
        centre
        + lat_coeff * (northern + southern - 2.0 * centre)
        + lon_coeff * (eastern + western - 2.0 * centre)
        - advect_coeff * centre * (eastern - western)
    )


def localize(obs_rows, rel_cols, first_row, row_count, lat_scale, width_cols):
    lower = first_row.astype(jnp.float32)
    upper = lower + row_count.astype(jnp.float32) - 1.0
    lat_gap = jnp.maximum(jnp.maximum(lower - obs_rows, obs_rows - upper), 0.0) / lat_scale
    lon_gap = jnp.maximum(jnp.maximum(-rel_cols, rel_cols - (width_cols - 1.0)), 0.0) / width_cols
    return jnp.exp(-lat_gap * lat_gap - lon_gap * lon_gap)


def dot3(left, right):
    return jnp.matmul(left, right, precision=lax.Precision.HIGH, preferred_element_type=jnp.float32)


def analyse(anomaly, state_mean, spread, obs_meta, lengths, width_cols):
    cell_total, members = anomaly.shape
    lat_total = cell_total // width_cols
    near = spread.shape[0]
    starts = jnp.cumsum(lengths) - lengths
    cell_rows = jnp.arange(cell_total, dtype=jnp.int32) // width_cols
    identity = jnp.eye(members, dtype=jnp.float32)
    products = dot3(spread, jnp.concatenate([spread, anomaly], axis=0).T)
    common, crossed = products[:, :near], products[:, near:]
    innov = obs_meta[0]
    shrink = jnp.zeros((cell_total,), jnp.float32)
    shift = state_mean
    weights_all = jnp.zeros((near, cell_total), jnp.float32)
    for patch in range(lengths.shape[0]):
        weights = (
            localize(obs_meta[2], obs_meta[3], starts[patch], lengths[patch], lat_total / 4.0, float(width_cols))
            / obs_meta[1]
        )
        scale = jnp.sqrt(weights)
        gram_matrix = (members - 1.0) * identity + jnp.dot(
            (spread * weights[:, None]).T, spread, preferred_element_type=jnp.float32
        )
        bound = jnp.max(jnp.sum(jnp.abs(gram_matrix), axis=1))
        alpha = (members - 1.0) / bound
        x = common * scale[:, None] * (scale / bound)[None, :]
        c0 = 2.25 + alpha * (-2.4375 + alpha * (1.6875 + alpha * (-0.5625 + alpha * 0.0625)))
        c1 = -2.4375 + alpha * (3.375 + alpha * (-1.6875 + alpha * 0.25))
        c2 = 1.6875 + alpha * (-1.6875 + alpha * 0.375)
        c3 = -0.5625 + alpha * 0.25
        c4 = 0.0625
        x2 = dot3(x, x)
        x34 = dot3(x2, jnp.concatenate([x, x2], axis=1))
        x3, x4 = x34[:, :near], x34[:, near:]
        low = c2 * x + c3 * x2 + c4 * x3
        high = c1 * x + c2 * x2 + c3 * x3 + c4 * x4
        block = jnp.concatenate([crossed * scale[:, None], (scale * innov)[:, None]], axis=1)
        both = dot3(jnp.concatenate([low, high], axis=0), block)
        b1 = c1 * block + both[:near]
        b2 = c0 * block + both[near:]
        b3 = c0 * b2 + dot3(high, b2)
        mixed = alpha * c0 * b1 + b3
        got = 1.5 * b1 - 0.5 * (
            alpha * c0 * c0 * b1
            + c0 * mixed
            + dot3(high, mixed)
            + alpha * (c1 * b3 + dot3(low, b3))
        )
        base = c0 * (1.5 - 0.5 * alpha * c0 * c0)
        driven = base * block[:, -1] + jnp.sum(x * got[:, -1][None, :], axis=1)
        again = jnp.sum(x * driven[None, :], axis=1)
        mean_part = (
            jnp.sum(block[:, :-1] * (base * driven)[:, None] + got[:, :-1] * again[:, None], axis=0)
            / bound
        )
        cell_mask = (cell_rows >= starts[patch]) & (cell_rows < starts[patch] + lengths[patch])
        root_scale = jnp.sqrt((members - 1.0) / bound)
        shift = shift + jnp.where(cell_mask, mean_part, 0.0)
        shrink = jnp.where(cell_mask, root_scale * base, shrink)
        weights_all = jnp.where(
            cell_mask[None, :], got[:, :-1] * (scale * (root_scale / bound))[:, None], weights_all
        )
    return shift[:, None] + shrink[:, None] * anomaly + dot3(weights_all.T, spread)


def general_device(ensemble, obs_cell, obs_value, obs_var, patch_rows):
    members_dev, lat_rows, lon_cells = ensemble.shape
    lat_count = lax.axis_size("lat")
    member_count = lax.axis_size("member")
    servers = lat_count * member_count
    width_cols = lon_cells // servers
    padded = with_halo(ensemble, (("lat", 1),), STEPS, False)
    global_rows = (
        lax.axis_index("lat") * lat_rows + jnp.arange(lat_rows + 2 * STEPS, dtype=jnp.int32) - STEPS
    )
    inside = ((global_rows >= 0) & (global_rows < lat_rows * lat_count)).astype(jnp.float32)
    for step_index in range(STEPS):
        padded = advance(padded)
        keeper = inside[step_index + 1 : inside.shape[0] - step_index - 1]
        padded = padded * keeper[None, :, None]
    blocks = padded.reshape(1, members_dev, lat_rows, lon_cells)
    received = lax.all_to_all(blocks, ("member", "lat"), split_axis=3, concat_axis=0, tiled=True)
    strip = received.reshape(member_count, lat_count, members_dev, lat_rows, width_cols)
    members = member_count * members_dev
    lat_total = lat_count * lat_rows
    states = strip.transpose(1, 3, 4, 0, 2).reshape(lat_total * width_cols, members)
    cell_index = obs_cell[0]
    obs_count = cell_index.shape[0]
    state_mean = jnp.mean(states, axis=1)
    anomaly = states - state_mean[:, None]
    spread = jnp.take(anomaly, cell_index, axis=0)
    innov = obs_value[0] - jnp.take(state_mean, cell_index)
    obs_meta = jnp.stack(
        [
            innov,
            obs_var[0],
            (cell_index // width_cols).astype(jnp.float32),
            (cell_index % width_cols).astype(jnp.float32),
        ]
    )
    near_spread = with_halo(spread, ((("member", "lat"), 0),), obs_count, True)
    near_meta = with_halo(obs_meta, ((("member", "lat"), 1),), obs_count, True)
    shifts = jnp.repeat(jnp.array([-1.0, 0.0, 1.0], jnp.float32), obs_count) * width_cols
    near_meta = jnp.concatenate([near_meta[:3], (near_meta[3] + shifts)[None, :]], axis=0)
    analysed = analyse(anomaly, state_mean, near_spread, near_meta, patch_rows[0], width_cols)
    outgoing = analysed.reshape(lat_count, lat_rows, width_cols, member_count, members_dev)
    outgoing = outgoing.transpose(3, 0, 4, 1, 2).reshape(servers, members_dev, lat_rows, width_cols)
    returned = lax.all_to_all(outgoing, ("member", "lat"), split_axis=0, concat_axis=3, tiled=True)
    return returned.reshape(members_dev, lat_rows, lon_cells)


def place(block, lats):
    half = block // (lats // 2)
    return (1 - half) * (2 * block) + half * (2 * lats - 1 - 2 * block)


def block_at(lat, lats):
    odd = lat % 2
    return (1 - odd) * (lat // 2) + odd * (lats - 1 - lat // 2)


def member_of(block, q, members):
    odd = block % 2
    return (1 - odd) * q + odd * (members - 1 - q)


def strip_at(m, lat, lats, members):
    block = block_at(lat, lats)
    return block * members + member_of(block, m, members)


def home_of(strip, lats, members):
    block = strip // members
    return member_of(block, strip % members, members), place(block, lats)


def greet_all(lats, members):
    m, lat = lax.axis_index("member"), lax.axis_index("lat")
    barrier = pltpu.get_barrier_semaphore()
    for dm in range(members):
        for dl in range(lats):
            if dm == 0 and dl == 0:
                continue
            pl.semaphore_signal(
                barrier, inc=1, device_id=((m + dm) % members, (lat + dl) % lats), device_id_type=MESH
            )
    return barrier, lats * members - 1


def forecast(load, lats, rows, groups):
    fields = [load(l) for l in range(lats)]
    lane = lax.broadcasted_iota(jnp.int32, fields[0].shape, 1)
    first, last = lane < groups, lane >= LANES - groups
    count = fields[0].shape[0]
    zero = jnp.zeros_like(fields[0])
    for _ in range(STEPS):
        new = []
        for l in range(lats):
            c = fields[l]
            above = fields[l - 1] if l > 0 else zero
            below = fields[l + 1] if l + 1 < lats else zero
            north = pltpu.roll(jnp.where(last, above, c), groups, 1)
            south = pltpu.roll(jnp.where(first, below, c), LANES - groups, 1)
            east = pltpu.roll(c, count - 1, 0)
            west = pltpu.roll(c, 1, 0)
            new.append(
                c
                + lat_coeff * (north + south - 2.0 * c)
                + lon_coeff * (east + west - 2.0 * c)
                - advect_coeff * c * (east - west)
            )
        fields = new
    return fields


def forward_kernel(
    dims, x_ref, obs_ref, at_ref, mean_ref, yt_ref, meta_ref,
    s_buf, ra, f_buf, r_buf, obs_buf, a_send, a_recv, b_send, b_recv, o_send, o_recv, y_send, y_recv,
):
    lats, members, chunks, rows, width, group = dims
    cols = width * members
    m, lat = lax.axis_index("member"), lax.axis_index("lat")
    barrier, partners = greet_all(lats, members)
    edge = STEPS

    for kc in range(chunks):
        whole = jnp.concatenate([x_ref[kc * group : (kc + 1) * group, r, :] for r in range(rows)], axis=0)
        turned = whole.T
        lon = turned.shape[0]
        for b in range(lats):
            s_buf[kc, b, 0:cols] = turned[b * cols : (b + 1) * cols]
            east, west = ((b + 1) * cols) % lon, (b * cols - edge) % lon
            s_buf[kc, b, cols : cols + edge] = turned[east : east + edge]
            s_buf[kc, b, cols + edge : cols + 2 * edge] = turned[west : west + edge]

    pl.semaphore_wait(barrier, partners)

    target_m, target_l = home_of(m * lats + lat, lats, members)
    away = jnp.logical_or(target_m != m, target_l != lat)
    obs_copy = pltpu.make_async_remote_copy(
        src_ref=obs_ref, dst_ref=obs_buf, send_sem=o_send, recv_sem=o_recv,
        device_id=(target_m, target_l), device_id_type=MESH,
    )

    @pl.when(away)
    def _():
        obs_copy.start()

    @pl.when(jnp.logical_not(away))
    def _():
        obs_buf[...] = obs_ref[...]

    a_copies = []
    for kc in range(chunks):
        for d in range(1, lats):
            to = (lat + d) % lats
            copy = pltpu.make_async_remote_copy(
                src_ref=s_buf.at[kc, block_at(to, lats)], dst_ref=ra.at[kc, lat],
                send_sem=a_send.at[kc, d], recv_sem=a_recv.at[kc, d],
                device_id=(m, to), device_id_type=MESH,
            )
            copy.start()
            a_copies.append(copy)

    own = block_at(lat, lats)
    own_odd = own % 2
    b_copies = []
    for kc in range(chunks):
        ra[kc, lat] = s_buf[kc, own]
        for copy in a_copies[kc * (lats - 1) : (kc + 1) * (lats - 1)]:
            copy.wait_recv()
        fields = forecast(lambda l, kc=kc: ra[kc, l], lats, rows, group)
        for l in range(lats):
            for q in range(members):
                f_buf[kc, q, l] = fields[l][q * width : (q + 1) * width]
        for d in range(1, members):
            to = (m + d) % members
            copy = pltpu.make_async_remote_copy(
                src_ref=f_buf.at[kc, member_of(own, to, members)], dst_ref=r_buf.at[m, kc],
                send_sem=b_send.at[kc, d], recv_sem=b_recv.at[kc, d],
                device_id=(to, lat), device_id_type=MESH,
            )
            copy.start()
            b_copies.append(copy)
        r_buf[m, kc] = f_buf[kc, member_of(own, m, members)]

    @pl.when(away)
    def _():
        obs_copy.wait_recv()

    for copy in b_copies:
        copy.wait_recv()

    per = LANES // group
    lane_block = lax.broadcasted_iota(jnp.int32, (lats * width, LANES), 1) // group
    total = members * chunks // per
    for g in range(total):
        parts = []
        for j in range(per):
            c = g * per + j
            parts.append(r_buf[c // chunks, c % chunks].reshape(lats * width, LANES))
        for r in range(rows):
            out = None
            for j in range(per):
                shift = (group * (j - r)) % LANES
                piece = pltpu.roll(parts[j], shift, 1) if shift else parts[j]
                out = piece if out is None else jnp.where(lane_block == j, piece, out)
            for l in range(lats):
                at_ref[(l * rows + r) * width : (l * rows + r + 1) * width, g * LANES : (g + 1) * LANES] = out[
                    l * width : (l + 1) * width
                ]
    states = at_ref[...]
    cells, count = states.shape
    mean = jnp.sum(states, axis=1, keepdims=True) * (1.0 / count)
    anomaly = states - mean
    at_ref[...] = anomaly
    mean_ref[...] = jnp.broadcast_to(mean, mean_ref.shape)

    nobs = obs_buf.shape[1]
    eye = (
        lax.broadcasted_iota(jnp.int32, (nobs, nobs), 0) == lax.broadcasted_iota(jnp.int32, (nobs, nobs), 1)
    ).astype(jnp.float32)
    cell_col = jnp.sum(eye * obs_buf[0:1, :], axis=1, keepdims=True)
    onehot = (
        cell_col == lax.broadcasted_iota(jnp.int32, (nobs, cells), 1).astype(jnp.float32)
    ).astype(jnp.float32)
    spread = jnp.dot(onehot, anomaly, precision=lax.Precision.HIGHEST, preferred_element_type=jnp.float32)
    hit = jnp.sum(
        (lax.broadcasted_iota(jnp.int32, (cells, nobs), 0).astype(jnp.float32) == obs_buf[0:1, :]).astype(jnp.float32)
        * mean,
        axis=0,
        keepdims=True,
    )
    cell_row = obs_buf[0:1, :]
    row = jnp.floor(cell_row * (1.0 / width))
    yt_ref[1] = spread
    meta_ref[1, 0:1, :] = obs_buf[1:2, :] - hit
    meta_ref[1, 1:2, :] = obs_buf[2:3, :]
    meta_ref[1, 2:3, :] = row
    meta_ref[1, 3:4, :] = cell_row - width * row
    meta_ref[1, 4:5, :] = obs_buf[3:4, :]
    meta_ref[1, 5:8, :] = jnp.zeros((3, nobs), jnp.float32)

    strip = strip_at(m, lat, lats, members)
    count_strips = lats * members
    y_copies = []
    for side, slot in ((1, 0), (count_strips - 1, 2)):
        to_m, to_l = home_of((strip + side) % count_strips, lats, members)
        for i, ref in enumerate((yt_ref, meta_ref)):
            copy = pltpu.make_async_remote_copy(
                src_ref=ref.at[1], dst_ref=ref.at[slot],
                send_sem=y_send.at[slot, i], recv_sem=y_recv.at[slot, i],
                device_id=(to_m, to_l), device_id_type=MESH,
            )
            copy.start()
            y_copies.append(copy)
    for copy in y_copies:
        copy.wait_recv()

    for copy in a_copies + b_copies + y_copies:
        copy.wait_send()

    @pl.when(away)
    def _():
        obs_copy.wait_send()


def forward(ensemble, obs, dims):
    lats, members, chunks, rows, width, group = dims
    cells, total = lats * rows * width, members * chunks * group
    nobs = obs.shape[1]
    dma = pltpu.SemaphoreType.DMA
    vmem = pl.BlockSpec(memory_space=pltpu.VMEM)
    f32 = jnp.float32
    return pl.pallas_call(
        functools.partial(forward_kernel, dims),
        out_shape=(
            jax.ShapeDtypeStruct((cells, total), f32),
            jax.ShapeDtypeStruct((cells, LANES), f32),
            jax.ShapeDtypeStruct((3, nobs, total), f32),
            jax.ShapeDtypeStruct((3, 8, nobs), f32),
        ),
        in_specs=[vmem, vmem],
        out_specs=[vmem] * 4,
        scratch_shapes=[
            pltpu.VMEM((chunks, lats, members * width + 2 * STEPS, LANES), f32),
            pltpu.VMEM((chunks, lats, members * width + 2 * STEPS, LANES), f32),
            pltpu.VMEM((chunks, members, lats, width, LANES), f32),
            pltpu.VMEM((members, chunks, lats, width, LANES), f32),
            pltpu.VMEM((8, nobs), f32),
            dma((chunks, lats)),
            dma((chunks, lats)),
            dma((chunks, members)),
            dma((chunks, members)),
            dma,
            dma,
            dma((3, 2)),
            dma((3, 2)),
        ],
        compiler_params=pltpu.CompilerParams(
            collective_id=0, has_side_effects=True, vmem_limit_bytes=48 * 1024 * 1024
        ),
        name="forward",
    )(ensemble, obs)


def backward_kernel(dims, y_ref, z_ref, t_buf, send, recv):
    lats, members, chunks, rows, width, group = dims
    m, lat = lax.axis_index("member"), lax.axis_index("lat")
    barrier, partners = greet_all(lats, members)
    per = LANES // group
    lane_block = lax.broadcasted_iota(jnp.int32, (lats * width, LANES), 1) // group
    for g in range(members * chunks // per):
        parts = []
        for r in range(rows):
            parts.append(
                jnp.concatenate(
                    [
                        y_ref[(l * rows + r) * width : (l * rows + r + 1) * width, g * LANES : (g + 1) * LANES]
                        for l in range(lats)
                    ],
                    axis=0,
                )
            )
        for j in range(per):
            c = g * per + j
            out = None
            for r in range(rows):
                shift = (group * (r - j)) % LANES
                piece = pltpu.roll(parts[r], shift, 1) if shift else parts[r]
                out = piece if out is None else jnp.where(lane_block == r, piece, out)
            for l in range(lats):
                t_buf[c // chunks, l, c % chunks] = out[l * width : (l + 1) * width]
    pl.semaphore_wait(barrier, partners)
    strip = strip_at(m, lat, lats, members)
    copies = []
    for dl in range(lats):
        for dm in range(members):
            if dm == 0 and dl == 0:
                continue
            to_m, to_l = (m + dm) % members, (lat + dl) % lats
            copy = pltpu.make_async_remote_copy(
                src_ref=t_buf.at[to_m, to_l], dst_ref=z_ref.at[strip],
                send_sem=send.at[dl, dm], recv_sem=recv.at[dl, dm],
                device_id=(to_m, to_l), device_id_type=MESH,
            )
            copy.start()
            copies.append(copy)
    z_ref[strip] = t_buf[m, lat]
    for copy in copies:
        copy.wait()


def backward(analysed, dims):
    lats, members, chunks, rows, width, group = dims
    dma = pltpu.SemaphoreType.DMA
    vmem = pl.BlockSpec(memory_space=pltpu.VMEM)
    f32 = jnp.float32
    return pl.pallas_call(
        functools.partial(backward_kernel, dims),
        out_shape=jax.ShapeDtypeStruct((lats * members, chunks, width, LANES), f32),
        in_specs=[vmem],
        out_specs=vmem,
        scratch_shapes=[
            pltpu.VMEM((members, lats, chunks, width, LANES), f32),
            dma((lats, members)),
            dma((lats, members)),
        ],
        compiler_params=pltpu.CompilerParams(
            collective_id=1, has_side_effects=True, vmem_limit_bytes=48 * 1024 * 1024
        ),
        name="backward",
    )(analysed)


def kernel_device(dims, ensemble, obs_cell, obs_value, obs_var, patch_rows):
    lats, members, chunks, rows, width, group = dims
    nobs = obs_cell.shape[1]
    obs = jnp.concatenate(
        [
            obs_cell.astype(jnp.float32),
            obs_value,
            obs_var,
            jnp.pad(patch_rows.astype(jnp.float32), ((0, 0), (0, nobs - patch_rows.shape[1]))),
            jnp.zeros((4, nobs), jnp.float32),
        ],
        axis=0,
    )
    anomaly, mean, spread, meta = forward(ensemble, obs, dims)
    lengths = meta[1, 4, : patch_rows.shape[1]].astype(jnp.int32)
    shifts = jnp.repeat(jnp.array([-1.0, 0.0, 1.0], jnp.float32), nobs) * width
    flat = meta[:, :4].transpose(1, 0, 2).reshape(4, 3 * nobs)
    near_meta = jnp.concatenate([flat[:3], (flat[3] + shifts)[None, :]], axis=0)
    near_spread = spread.reshape(3 * nobs, spread.shape[2])
    analysed = analyse(anomaly, mean[:, 0], near_spread, near_meta, lengths, width)
    pieces = backward(analysed, dims)
    strips = lats * members
    return (
        pieces.reshape(strips, chunks, width, rows, group)
        .transpose(1, 4, 3, 0, 2)
        .reshape(chunks * group, rows, strips * width)
    )


def kernel_dims(mesh, ensemble, obs_cell, patch_rows):
    lats, members = mesh.shape["lat"], mesh.shape["member"]
    total, lat_all, lon = ensemble.shape
    own, rows = total // members, lat_all // lats
    width = lon // (lats * members)
    if LANES % rows:
        return None
    group = LANES // rows
    fits = (
        own % group == 0
        and (members * (own // group)) % rows == 0
        and width == 8
        and lats % 2 == 0
        and members % 2 == 0
        and obs_cell.shape[1] % LANES == 0
        and patch_rows.shape[1] == 2
    )
    return (lats, members, own // group, rows, width, group) if fits else None


def solution(mesh):
    specs = (P("member", "lat", None),) + (P(("member", "lat"), None),) * 4

    def run(ensemble, obs_cell, obs_value, obs_var, patch_rows):
        dims = kernel_dims(mesh, ensemble, obs_cell, patch_rows)
        body = general_device if dims is None else functools.partial(kernel_device, dims)
        mapped = jax.shard_map(
            body, mesh=mesh, in_specs=specs, out_specs=P("member", "lat", None), check_vma=False
        )
        return mapped(ensemble, obs_cell, obs_value, obs_var, patch_rows)

    return run
```

time: 165 us -> 139 us (0.84)
  the two profiles are of different devices: /device:TPU:0 before, /device:TPU:11 now
where the time goes in v1:
time: 139 us; the launch traced here: 138 us
  Pallas kernels  55.8 us (40%)
  matrix products  31.9 us (23%)
  local copies, waits for them, and re-layouts  21.9 us (16%)
  other arithmetic  20.1 us (14%)
  between operations  8.28 us (6%)
    pallas_call x1, Pallas kernels, forward(): pl.pallas_call(functools.partial(forward_kernel, dims), out_shape=(jax.Sh...  35.6 us
    dot_general x14, matrix products, dot3(): jnp.matmul(left, right, precision=lax.Precision.HIGH, preferred_element_t...  30.5 us
    pallas_call x1, Pallas kernels, backward(): pl.pallas_call(functools.partial(backward_kernel, dims), out_shape=jax.Sh...  20.1 us
    reshape x2, local copies, waits for them, and re-layouts, kernel_device(): pieces.reshape(strips, chunks, width, rows, group).transpose(1, 4, 3, 0, 2)  7.93 us
    add x2, other arithmetic, analyse(): high = c1 * x + c2 * x2 + c3 * x3 + c4 * x4  5.14 us
    unnamed x42, local copies, waits for them, and re-layouts  4.4 us
    reshape x2, local copies, waits for them, and re-layouts, kernel_device(): return pieces.reshape(strips, chunks, width, rows, group).transpose(1, 4,...  4.32 us

profile of v1, /device:TPU:11, one launch (start us, length us, event | category | flops | bytes accessed | tf_op | source)
XLA Modules:
  0.0 137.9 jit_solution(14287247590851776505)
XLA Ops:
  2.0 1.1 copy-done
  3.1 35.6 %forward.1 = (f32[256,640]{1,0:T(8,128)S(1)}, f32[256,128]{1,0:T(8,128)S(1)}, f32[3,128,640]{2,1,0:T(8,128)S(1)}, f32[3,8,128]{2,1,0:T(8,128)S(1)}) custom-call(f32[160,4,256]{2,1,0:T(4,128)S(1)} %copy-done, f32[8,128]{1,0:T(8,128)S(1)} %concatenate.24.obs_ref), custom_call_target="tpu_custom_call" | custom-call | tf_op jit(solution)/shard_map/forward/pallas_call | solution.py:392
  38.8 2.5 %fusion.4 = f32[384,640]{1,0:T(8,128)} fusion(f32[384,640]{1,0:T(8,128)S(1)} %bitcast.153, f32[256,640]{1,0:T(8,128)S(1)} %get-tuple-element.12), kind=kOutput, calls=%fused_computation.7 | convolution fusion | flops 944128000 | bytes 2621440 | tf_op jit(solution)/shard_map/dot_general | solution.py:56
  53.0 1.4 %broadcast_divide_fusion = (f32[384]{0:T(512)S(1)}, f32[384]{0:T(512)S(1)}) fusion(f32[384]{0:T(512)S(1)} %get-tuple-element.42, f32[]{:T(128)} %reduce_max.19, f32[384]{0:T(512)S(1)} %get-tuple-element.18, f32[]{:T(128)} %reduce_max.18), kind=kLoop, calls=%fused_computation.170 | loop fusion | flops 768 | bytes 6152 | tf_op jit(solution)/shard_map/div | solution.py:83
  54.4 1.2 multiply_multiply_fusion.1
  56.3 2.1 %fusion.26 = f32[384,768]{1,0:T(8,128)} fusion(f32[384,384]{1,0:T(8,128)S(1)} %fusion.120, f32[384,384]{1,0:T(8,128)S(1)} %get-tuple-element.35), kind=kOutput, calls=%fused_computation.37 | convolution fusion | flops 679772160 | bytes 2359296 | tf_op jit(solution)/shard_map/dot_general | solution.py:56
  58.5 2.5 %fusion.34 = (f32[384,384]{1,0:T(8,128)}, f32[384,384]{1,0:T(8,128)}) fusion(f32[384,768]{1,0:T(8,128)} %fusion.26, f32[384,384]{1,0:T(8,128)S(1)} %fusion.120, f32[384,384]{1,0:T(8,128)S(1)} %get-tuple-element.35, f32[]{:T(128)S(6)} %add.375, f32[]{:T(128)S(6)} %add.378, f32[]{:T(128)S(6)} %add.377), kind=kLoop, calls=%fused_computation.48 | loop fusion | flops 1769472 | bytes 3538956 | tf_op jit(solution)/shard_map/add | solution.py:93
  61.7 1.3 slice_multiply_fusion.3
  63.8 2.2 %fusion.30 = f32[768,257]{1,0:T(8,128)} fusion(f32[384,384]{1,0:T(8,128)S(1)} %copy-done.3, f32[384,384]{1,0:T(8,128)S(1)} %copy-done.4, f32[384,1]{1,0:T(8,128)S(1)} %copy.71, f32[384,256]{1,0:T(8,128)S(1)} %get-tuple-element.33), kind=kOutput, calls=%fused_computation.41 | convolution fusion | flops 455147904 | bytes 2363904 | tf_op jit(solution)/shard_map/dot_general | solution.py:56
  66.0 2.4 %convolution_add_fusion.3 = f32[384,257]{1,0:T(8,128)S(1)} fusion(f32[384,384]{1,0:T(8,128)} %get-tuple-element.30, f32[768,257]{1,0:T(8,128)} %fusion.30, f32[384,1]{1,0:T(8,128)S(1)} %copy.71, f32[384,256]{1,0:T(8,128)} %copy-done.1, f32[]{:T(128)S(6)} %add.372), kind=kOutput, calls=%fused_computation.17 | convolution fusion | flops 228166656 | bytes 3344896 | tf_op jit(solution)/shard_map/dot_general | solution.py:56
  68.5 0.8 copy-done.8
  69.3 1.7 %fusion.17 = f32[384,257]{1,0:T(8,128)} fusion(f32[384,384]{1,0:T(8,128)S(1)} %copy-done.5, f32[384,257]{1,0:T(8,128)S(1)} %convolution_add_fusion.3, f32[]{:T(128)S(6)} %div.205, f32[]{:T(128)S(6)} %add.375), kind=kOutput, calls=%fused_computation.28 | convolution fusion | flops 227673216 | bytes 1379336 | tf_op jit(solution)/shard_map/dot_general | solution.py:56
  71.0 4.0 %fusion.16 = f32[384,257]{1,0:T(8,128)} fusion(f32[384,257]{1,0:T(8,128)} %fusion.17, f32[384,384]{1,0:T(8,128)} %get-tuple-element.30, f32[384,257]{1,0:T(8,128)} %copy-done.8, f32[768,257]{1,0:T(8,128)} %fusion.30, f32[384,1]{1,0:T(8,128)S(1)} %copy.71, f32[384,256]{1,0:T(8,128)} %copy-done.1, f32[]{:T(128)S(6)} %mul.822, f32[]{:T(128)S(6)} %add.372, ...), kind=kOutput, calls=%fused_computation.27 | convolution fusion | flops 229153536 | bytes 5116416 | tf_op jit(solution)/shard_map/dot_general | solution.py:56
  75.7 0.8 copy-done.7
  76.5 2.1 %fusion.18 = f32[384,768]{1,0:T(8,128)} fusion(f32[384,384]{1,0:T(8,128)S(1)} %fusion.119, f32[384,384]{1,0:T(8,128)S(1)} %get-tuple-element.34), kind=kOutput, calls=%fused_computation.29 | convolution fusion | flops 679772160 | bytes 2359296 | tf_op jit(solution)/shard_map/dot_general | solution.py:56
  78.6 2.7 %fusion.35 = (f32[384,384]{1,0:T(8,128)}, f32[384,384]{1,0:T(8,128)}) fusion(f32[384,768]{1,0:T(8,128)} %fusion.18, f32[384,384]{1,0:T(8,128)} %copy-done.7, f32[384,384]{1,0:T(8,128)S(1)} %get-tuple-element.34, f32[]{:T(128)S(6)} %add.345, f32[]{:T(128)S(6)} %add.349, f32[]{:T(128)S(6)} %add.348), kind=kLoop, calls=%fused_computation.52 | loop fusion | flops 1769472 | bytes 3538956 | tf_op jit(solution)/shard_map/add | solution.py:93
  81.4 3.5 %fusion.22 = f32[768,257]{1,0:T(8,128)} fusion(f32[384,384]{1,0:T(8,128)} %get-tuple-element.28, f32[384,384]{1,0:T(8,128)} %get-tuple-element.29, f32[384,1]{1,0:T(8,128)S(1)} %copy.63, f32[384,256]{1,0:T(8,128)S(1)} %get-tuple-element.32), kind=kOutput, calls=%fused_computation.33 | convolution fusion | flops 455147904 | bytes 2363904 | tf_op jit(solution)/shard_map/dot_general | solution.py:56
  84.9 2.2 %convolution_add_fusion.6 = f32[384,257]{1,0:T(8,128)S(1)} fusion(f32[384,384]{1,0:T(8,128)} %get-tuple-element.28, f32[768,257]{1,0:T(8,128)} %fusion.22, f32[384,1]{1,0:T(8,128)S(1)} %copy.63, f32[384,256]{1,0:T(8,128)S(1)} %get-tuple-element.32, f32[]{:T(128)S(6)} %add.342), kind=kOutput, calls=%fused_computation.20 | convolution fusion | flops 228166656 | bytes 2954752 | tf_op jit(solution)/shard_map/dot_general | solution.py:56
  87.1 0.8 copy-done.9
  88.0 1.5 %fusion.13 = f32[384,257]{1,0:T(8,128)} fusion(f32[384,384]{1,0:T(8,128)S(1)} %copy-done.6, f32[384,257]{1,0:T(8,128)S(1)} %convolution_add_fusion.6, f32[]{:T(128)S(6)} %div.191, f32[]{:T(128)S(6)} %add.345), kind=kOutput, calls=%fused_computation.24 | convolution fusion | flops 227673216 | bytes 1379336 | tf_op jit(solution)/shard_map/dot_general | solution.py:56
  89.5 3.8 %fusion.12 = f32[384,257]{1,0:T(8,128)} fusion(f32[384,257]{1,0:T(8,128)} %fusion.13, f32[384,384]{1,0:T(8,128)} %get-tuple-element.28, f32[384,257]{1,0:T(8,128)} %copy-done.9, f32[768,257]{1,0:T(8,128)} %fusion.22, f32[384,1]{1,0:T(8,128)S(1)} %copy.63, f32[384,256]{1,0:T(8,128)S(1)} %get-tuple-element.32, f32[]{:T(128)S(6)} %mul.757, f32[]{:T(128)S(6)} %add.342, ...), kind=kOutput, calls=%fused_computation.23 | convolution fusion | flops 229153536 | bytes 5116416 | tf_op jit(solution)/shard_map/dot_general | solution.py:56
  95.8 1.3 select_select_fusion
  97.1 1.1 slice_reduce_fusion.1
  98.3 1.1 slice_reduce_fusion
  101.0 1.2 add_reduce_fusion.1
  103.1 1.4 %add_reduce_fusion.2 = f32[256]{0:T(256)S(1)} fusion(f32[256,1]{1,0:T(8,128)S(1)} %copy.77, f32[256,1]{1,0:T(8,128)S(1)} %copy.69, f32[256,128]{1,0:T(8,128)S(1)} %get-tuple-element.9, s32[]{:T(128)S(6)} %add.366, s32[]{:T(128)} %bitcast.16, s32[]{:T(128)S(6)} %add.334, s32[]{:T(128)} %bitcast.3), kind=kLoop, calls=%fused_computation.106 | loop fusion | flops 4608 | bytes 4112 | tf_op jit(solution)/shard_map/add | solution.py:115
  104.5 1.0 convolution_add_fusion.y_ref
  105.5 20.1 %backward.1 = f32[32,5,8,128]{3,2,1,0:T(8,128)S(1)} custom-call(f32[256,640]{1,0:T(8,128)S(1)} %convolution_add_fusion.y_ref), custom_call_target="tpu_custom_call" | custom-call | tf_op jit(solution)/shard_map/backward/pallas_call | solution.py:476
  125.7 2.6 %reshape.647 = f32[32,5,8,4,32]{4,3,2,1,0:T(4,128)} reshape(f32[32,5,8,128]{3,2,1,0:T(8,128)S(1)} %backward.1) | data formatting | bytes 1310720 | tf_op jit(solution)/shard_map/reshape | solution.py:516
  128.3 5.3 %copy.163 = f32[32,5,8,4,32]{4,1,2,0,3:T(8,128)} copy(f32[32,5,8,4,32]{4,3,2,1,0:T(4,128)} %reshape.647) | data formatting | bytes 1310720 | tf_op jit(solution)/shard_map/reshape | solution.py:516
  133.6 3.2 %reshape.648 = f32[160,4,256]{0,2,1:T(8,128)S(1)} reshape(f32[5,32,4,32,8]{1,0,4,3,2:T(8,128)} %bitcast.155) | data formatting | bytes 1310720 | tf_op jit(solution)/shard_map/reshape | solution.py:518
  136.8 1.1 copy.79
  (73 shorter events, 13.9 us)
Async XLA Ops:
  2.0 1.1 copy-start
  38.8 7.0 %copy-start.20 = (f32[3]{0:T(128)S(1)}, f32[3]{0:T(128)}, u32[]{:S(2)}) copy-start(f32[3]{0:T(128)} %constant.89) | copy-start | bytes 40
  41.9 10.4 %copy-start.13 = (f32[1,3,128]{2,0,1:T(1,128)}, f32[1,3,128]{2,0,1:T(1,128)S(1)}, u32[]{:S(2)}) copy-start(f32[1,3,128]{2,0,1:T(1,128)S(1)} %get-tuple-element.38) | copy-start | bytes 4612
  58.4 2.5 %copy-start.14 = (f32[1,3,128]{2,0,1:T(1,128)S(1)}, f32[1,3,128]{2,0,1:T(1,128)}, u32[]{:S(2)}) copy-start(f32[1,3,128]{2,0,1:T(1,128)} %copy-done.13) | copy-start | bytes 4612
  58.4 2.5 %copy-start.18 = (f32[1,1,3,128]{3,2,1,0:T(4,128)S(1)}, f32[1,1,3,128]{3,2,1,0:T(4,128)}, u32[]{:S(2)}) copy-start(f32[1,1,3,128]{3,2,1,0:T(4,128)} %get-tuple-element.49) | copy-start | bytes 4612
  61.7 2.0 %copy-start.3 = (f32[384,384]{1,0:T(8,128)S(1)}, f32[384,384]{1,0:T(8,128)}, u32[]{:S(2)}) copy-start(f32[384,384]{1,0:T(8,128)} %get-tuple-element.30) | copy-start | bytes 1769476
  61.7 2.0 %copy-start.4 = (f32[384,384]{1,0:T(8,128)S(1)}, f32[384,384]{1,0:T(8,128)}, u32[]{:S(2)}) copy-start(f32[384,384]{1,0:T(8,128)} %get-tuple-element.31) | copy-start | bytes 1769476
  63.0 0.8 copy-start.1
  66.0 3.3 %copy-start.5 = (f32[384,384]{1,0:T(8,128)S(1)}, f32[384,384]{1,0:T(8,128)}, u32[]{:S(2)}) copy-start(f32[384,384]{1,0:T(8,128)} %get-tuple-element.31) | copy-start | bytes 1769476
  68.4 0.8 copy-start.8
  75.7 0.8 copy-start.7
  78.6 2.7 %copy-start.19 = (f32[384,1]{0,1:T(1,128)S(1)}, f32[384,1]{0,1:T(1,128)}, u32[]{:S(2)}) copy-start(f32[384,1]{0,1:T(1,128)} %get-tuple-element.26) | copy-start | bytes 4612
  84.9 3.1 %copy-start.6 = (f32[384,384]{1,0:T(8,128)S(1)}, f32[384,384]{1,0:T(8,128)}, u32[]{:S(2)}) copy-start(f32[384,384]{1,0:T(8,128)} %get-tuple-element.29) | copy-start | bytes 1769476
  87.1 0.8 copy-start.9
  93.3 6.3 %copy-start.17 = (f32[3,128]{1,0:T(4,128)S(1)}, f32[3,128]{1,0:T(4,128)}, u32[]{:S(2)}) copy-start(f32[3,128]{1,0:T(4,128)} %get-tuple-element.13) | copy-start | bytes 4612
  95.7 4.0 %copy-start.2 = (f32[384,256]{1,0:T(8,128)S(1)}, f32[384,256]{1,0:T(8,128)}, u32[]{:S(2)}) copy-start(f32[384,256]{1,0:T(8,128)} %copy-done.1) | copy-start | bytes 1179652
  95.8 4.0 %copy-start.10 = (f32[384,257]{1,0:T(8,128)S(1)}, f32[384,257]{1,0:T(8,128)}, u32[]{:S(2)}) copy-start(f32[384,257]{1,0:T(8,128)} %fusion.16) | copy-start | bytes 1184260
  99.9 4.6 %copy-start.11 = (f32[384,257]{1,0:T(8,128)S(1)}, f32[384,257]{1,0:T(8,128)}, u32[]{:S(2)}) copy-start(f32[384,257]{1,0:T(8,128)} %fusion.16) | copy-start | bytes 1184260
  99.9 4.6 %copy-start.15 = (f32[384]{0:T(512)S(1)}, f32[384]{0:T(512)}, u32[]{:S(2)}) copy-start(f32[384]{0:T(512)} %get-tuple-element.17) | copy-start | bytes 4612
  100.0 4.6 %copy-start.16 = (f32[384]{0:T(512)S(1)}, f32[384]{0:T(512)}, u32[]{:S(2)}) copy-start(f32[384]{0:T(512)} %get-tuple-element.41) | copy-start | bytes 4612
  101.0 3.5 %copy-start.12 = (f32[384,257]{1,0:T(8,128)S(1)}, f32[384,257]{1,0:T(8,128)}, u32[]{:S(2)}) copy-start(f32[384,257]{1,0:T(8,128)} %fusion.12) | copy-start | bytes 1184260

commit v2 on v1

--- a/solution.py
+++ b/solution.py
@@ -490,6 +490,143 @@
     )(analysed)
 
 
+def split(a):
+    high = a.astype(jnp.bfloat16)
+    return high, (a - high.astype(jnp.float32)).astype(jnp.bfloat16)
+
+
+def dot_pairs(a, b, dims=(((1,), (0,)), ((), ()))):
+    (ah, al), (bh, bl) = a, b
+    one = functools.partial(lax.dot_general, dimension_numbers=dims, preferred_element_type=jnp.float32)
+    return one(ah, bh) + (one(ah, bl) + one(al, bh))
+
+
+def to_column(row):
+    eye = lax.broadcasted_iota(jnp.int32, (LANES, LANES), 0) == lax.broadcasted_iota(jnp.int32, (LANES, LANES), 1)
+    return jnp.concatenate(
+        [
+            jnp.sum(jnp.where(eye, row[:, i : i + LANES], 0.0), axis=1, keepdims=True)
+            for i in range(0, row.shape[1], LANES)
+        ],
+        axis=0,
+    )
+
+
+def analysis(dims, at, mean, yt, meta):
+    lats, members, chunks, rows, width, group = dims
+    cells, count = at.shape
+    near = yt.shape[0]
+    side = near // 3
+    lat_total = cells // width
+    y_pair = split(yt)
+    a_pair = split(at)
+    across = (((1,), (1,)), ((), ()))
+    common = dot_pairs(y_pair, y_pair, across)
+    crossed = dot_pairs(y_pair, a_pair, across)
+    y_turned = yt.T
+
+    strip_of = lax.broadcasted_iota(jnp.int32, (1, near), 1) // side - 1
+    innov, var, obs_rows = meta[0:1], meta[1:2], meta[2:3]
+    cols = meta[3:4] + (strip_of * width).astype(jnp.float32)
+    lengths = [meta[4:5, side + i : side + i + 1] for i in range(2)]
+    starts = [jnp.zeros_like(lengths[0]), lengths[0]]
+    lon_gap = jnp.maximum(jnp.maximum(-cols, cols - (width - 1.0)), 0.0) / float(width)
+    cell_row_lane = (lax.broadcasted_iota(jnp.int32, (1, cells), 1) // width).astype(jnp.float32)
+    cell_row_col = (lax.broadcasted_iota(jnp.int32, (cells, 1), 0) // width).astype(jnp.float32)
+    lane = lax.broadcasted_iota(jnp.int32, (near, cells), 1)
+
+    shift = jnp.zeros((1, cells), jnp.float32)
+    shrink = jnp.zeros((cells, 1), jnp.float32)
+    combined = None
+    for patch in range(2):
+        lower = starts[patch]
+        upper = lower + lengths[patch] - 1.0
+        lat_gap = jnp.maximum(jnp.maximum(lower - obs_rows, obs_rows - upper), 0.0) / (lat_total / 4.0)
+        weights = jnp.exp(-lat_gap * lat_gap - lon_gap * lon_gap) / var
+        scale = jnp.sqrt(weights)
+        left = (y_turned * weights).astype(jnp.bfloat16)
+        sums = None
+        for i in range(0, count, LANES):
+            tile = jnp.abs(jnp.dot(left[i : i + LANES], y_pair[0], preferred_element_type=jnp.float32))
+            part = jnp.sum(tile, axis=0, keepdims=True)
+            sums = part if sums is None else sums + part
+        bound = (count - 1.0) + jnp.max(sums, axis=1, keepdims=True)
+        inverse = 1.0 / bound
+        alpha = (count - 1.0) * inverse
+        scale_col = to_column(scale)
+        x = common * scale_col * (scale * inverse)
+        c0 = 2.25 + alpha * (-2.4375 + alpha * (1.6875 + alpha * (-0.5625 + alpha * 0.0625)))
+        c1 = -2.4375 + alpha * (3.375 + alpha * (-1.6875 + alpha * 0.25))
+        c2 = 1.6875 + alpha * (-1.6875 + alpha * 0.375)
+        c3 = -0.5625 + alpha * 0.25
+        c4 = 0.0625
+        x_pair = split(x)
+        x2 = dot_pairs(x_pair, x_pair)
+        low = c2 * x + c3 * x2 + c4 * dot_pairs(split(x2), x_pair)
+        low_pair = split(low)
+        spare = cells - 1 if patch == 0 else 0
+        block = jnp.where(lane == spare, to_column(innov), crossed) * scale_col
+        b_pair = split(block)
+        b1 = c1 * block + dot_pairs(low_pair, b_pair)
+        b2 = c0 * block + dot_pairs(x_pair, split(b1))
+        w = c1 * b2 + dot_pairs(low_pair, split(b2))
+        b3 = c0 * b2 + dot_pairs(x_pair, split(w))
+        u = c1 * b3 + dot_pairs(low_pair, split(b3))
+        z = c0 * b3 + dot_pairs(x_pair, split(u))
+        got = 1.5 * b1 - 0.5 * (z + alpha * (u + c0 * (w + c0 * b1)))
+        base = c0 * (1.5 - 0.5 * alpha * c0 * c0)
+        full = base * block + dot_pairs(x_pair, split(got))
+        drive = full[:, spare : spare + 1]
+        mean_part = jnp.sum(full * drive, axis=0, keepdims=True) * inverse
+        root_scale = jnp.sqrt(alpha)
+        inside = jnp.logical_and(cell_row_lane >= lower, cell_row_lane <= upper)
+        inside_col = jnp.logical_and(cell_row_col >= lower, cell_row_col <= upper)
+        shift = jnp.where(inside, mean_part, shift)
+        shrink = jnp.where(inside_col, root_scale * base, shrink)
+        weighted = got * (scale_col * (root_scale * inverse))
+        combined = weighted if combined is None else jnp.where(inside, weighted, combined)
+    return (mean + to_column(shift)) + shrink * at + dot_pairs(split(combined.T), y_pair)
+
+
+def analysis_kernel(dims, at_ref, mean_ref, yt_ref, meta_ref, out_ref):
+    yt = jnp.concatenate([yt_ref[i] for i in range(3)], axis=0)
+    meta = jnp.concatenate([meta_ref[i] for i in range(3)], axis=1)
+    out_ref[...] = analysis(dims, at_ref[...], mean_ref[:, 0:1], yt, meta)
+
+
+def analyse_strip(anomaly, mean, spread, meta, dims):
+    vmem = pl.BlockSpec(memory_space=pltpu.VMEM)
+    return pl.pallas_call(
+        functools.partial(analysis_kernel, dims),
+        out_shape=jax.ShapeDtypeStruct(anomaly.shape, jnp.float32),
+        in_specs=[vmem] * 4,
+        out_specs=vmem,
+        compiler_params=pltpu.CompilerParams(vmem_limit_bytes=56 * 1024 * 1024),
+        name="analysis",
+    )(anomaly, mean, spread, meta)
+
+
+def settle_kernel(dims, z_ref, out_ref):
+    lats, members, chunks, rows, width, group = dims
+    for kc in range(chunks):
+        lon = jnp.concatenate([z_ref[s, kc] for s in range(lats * members)], axis=0)
+        turned = lon.T
+        for r in range(rows):
+            out_ref[kc * group : (kc + 1) * group, r, :] = turned[r * group : (r + 1) * group]
+
+
+def settle(pieces, dims):
+    lats, members, chunks, rows, width, group = dims
+    vmem = pl.BlockSpec(memory_space=pltpu.VMEM)
+    return pl.pallas_call(
+        functools.partial(settle_kernel, dims),
+        out_shape=jax.ShapeDtypeStruct((chunks * group, rows, lats * members * width), jnp.float32),
+        in_specs=[vmem],
+        out_specs=vmem,
+        name="settle",
+    )(pieces)
+
+
 def kernel_device(dims, ensemble, obs_cell, obs_value, obs_var, patch_rows):
     lats, members, chunks, rows, width, group = dims
     nobs = obs_cell.shape[1]
@@ -504,19 +641,8 @@
         axis=0,
     )
     anomaly, mean, spread, meta = forward(ensemble, obs, dims)
-    lengths = meta[1, 4, : patch_rows.shape[1]].astype(jnp.int32)
-    shifts = jnp.repeat(jnp.array([-1.0, 0.0, 1.0], jnp.float32), nobs) * width
-    flat = meta[:, :4].transpose(1, 0, 2).reshape(4, 3 * nobs)
-    near_meta = jnp.concatenate([flat[:3], (flat[3] + shifts)[None, :]], axis=0)
-    near_spread = spread.reshape(3 * nobs, spread.shape[2])
-    analysed = analyse(anomaly, mean[:, 0], near_spread, near_meta, lengths, width)
-    pieces = backward(analysed, dims)
-    strips = lats * members
-    return (
-        pieces.reshape(strips, chunks, width, rows, group)
-        .transpose(1, 4, 3, 0, 2)
-        .reshape(chunks * group, rows, strips * width)
-    )
+    analysed = analyse_strip(anomaly, mean, spread, meta, dims)
+    return settle(backward(analysed, dims), dims)
 
 
 def kernel_dims(mesh, ensemble, obs_cell, patch_rows):

time: 139 us -> 83.9 us (0.60)
  matrix products: 31.9 us -> 0 us
  Pallas kernels: 55.8 us -> 76.1 us
  other arithmetic: 20.1 us -> 0.67 us
  local copies, waits for them, and re-layouts: 21.9 us -> 6.71 us
  between operations: 8.28 us -> 0.07 us
    dot_general x16 -> x0, matrix products: 31.9 us -> none  [the longest x14 30.5 us: dot3(): jnp.matmul(left, right, precision=lax.Precision.HIGH, preferred_element_t...]
    pallas_call x0 -> x2, Pallas kernels: none -> 20.5 us  [the longest x1 18.3 us: analyse_strip(): pl.pallas_call(functools.partial(analysis_kernel, dims), out_shape=jax.Sh...]
    reshape x4 -> x0, local copies, waits for them, and re-layouts: 12.2 us -> none  [the longest x2 7.93 us: kernel_device(): pieces.reshape(strips, chunks, width, rows, group).transpose(1, 4, 3, 0, 2)]
    add x3 -> x0, other arithmetic: 6.53 us -> none  [the longest x2 5.14 us: analyse(): high = c1 * x + c2 * x2 + c3 * x3 + c4 * x4]
    slice x5 -> x0, local copies, waits for them, and re-layouts: 3.98 us -> none  [the longest x2 2.14 us: analyse(): driven = base * block[:, -1] + jnp.sum(x * got[:, -1][None, :], axis=1)]
    mul x6 -> x0, other arithmetic: 3.79 us -> none  [the longest x1 1.26 us: analyse(): crossed * scale[:, None]]
    div x4 -> x0, other arithmetic: 3.48 us -> none  [the longest x2 1.45 us: analyse(): jnp.sum(block[:, :-1] * (base * driven)[:, None] + got[:, :-1] * again[:,...]
    unnamed x42 -> x20, local copies, waits for them, and re-layouts: 4.4 us -> 6.68 us
where the time goes in v2:
time: 83.9 us; the launch traced here: 83.6 us
  Pallas kernels  76.1 us (91%)
  local copies, waits for them, and re-layouts  6.71 us (8%)
    pallas_call x1, Pallas kernels, forward(): pl.pallas_call(functools.partial(forward_kernel, dims), out_shape=(jax.Sh...  35.6 us
    pallas_call x1, Pallas kernels, backward(): pl.pallas_call(functools.partial(backward_kernel, dims), out_shape=jax.Sh...  19.9 us
    pallas_call x1, Pallas kernels, analyse_strip(): pl.pallas_call(functools.partial(analysis_kernel, dims), out_shape=jax.Sh...  18.3 us
    unnamed x20, local copies, waits for them, and re-layouts  6.68 us
    pallas_call x1, Pallas kernels, settle(): pl.pallas_call(functools.partial(settle_kernel, dims), out_shape=jax.Shap...  2.18 us

profile of v2, /device:TPU:11, one launch (start us, length us, event | category | flops | bytes accessed | tf_op | source)
XLA Modules:
  0.0 83.6 jit_solution(17533061252627583513)
XLA Ops:
  0.0 0.0 copy-start.9
  0.0 0.7 convert_element_type.8
  0.7 0.0 copy-done.9
  0.7 0.0 copy-start.7
  0.7 0.0 copy-start.8
  0.7 0.6 copy-done.7
  1.3 0.0 copy-done.8
  1.4 0.0 copy-start.3
  1.4 1.1 %copy-done.3 = f32[160,4,256]{2,1,0:T(4,128)S(1)} copy-done((f32[160,4,256]{2,1,0:T(4,128)S(1)}, f32[160,4,256]{2,1,0:T(4,128)}, u32[]{:S(2)}) %copy-start.3) | copy-done | bytes 655384
  2.5 35.6 %forward.1 = (f32[256,640]{1,0:T(8,128)S(1)}, f32[256,128]{1,0:T(8,128)S(1)}, f32[3,128,640]{2,1,0:T(8,128)S(1)}, f32[3,8,128]{2,1,0:T(8,128)S(1)}) custom-call(f32[160,4,256]{2,1,0:T(4,128)S(1)} %copy-done.3, f32[8,128]{1,0:T(8,128)S(1)} %concatenate.3.obs_ref), custom_call_target="tpu_custom_call" | custom-call | tf_op jit(solution)/shard_map/forward/pallas_call | solution.py:392
  38.1 0.0 copy-start.2
  38.1 0.9 %copy-done.2 = f32[3,128,640]{2,1,0:T(8,128)} copy-done((f32[3,128,640]{2,1,0:T(8,128)}, f32[3,128,640]{2,1,0:T(8,128)S(1)}, u32[]{:S(2)}) %copy-start.2) | copy-done | bytes 983064
  39.1 0.0 copy-start.4
  39.1 0.8 copy-done.4
  39.9 0.0 copy-start.5
  39.9 0.6 copy-done.5
  40.6 0.0 copy-start.6
  40.6 0.6 copy-done.6
  41.1 18.3 %analysis.1.y_ref = f32[256,640]{1,0:T(8,128)} custom-call(f32[256,640]{1,0:T(8,128)} %copy-done.4, f32[256,128]{1,0:T(8,128)} %copy-done.5, f32[3,128,640]{2,1,0:T(8,128)} %copy-done.2, f32[3,8,128]{2,1,0:T(8,128)} %copy-done.6), custom_call_target="tpu_custom_call" | custom-call | tf_op jit(solution)/shard_map/analysis/pallas_call | solution.py:599
  59.5 0.0 copy-start.1
  59.5 1.1 %copy-done.1 = f32[256,640]{1,0:T(8,128)S(1)} copy-done((f32[256,640]{1,0:T(8,128)S(1)}, f32[256,640]{1,0:T(8,128)}, u32[]{:S(2)}) %copy-start.1) | copy-done | bytes 655384
  60.6 19.9 %backward.1.z_ref = f32[32,5,8,128]{3,2,1,0:T(8,128)S(1)} custom-call(f32[256,640]{1,0:T(8,128)S(1)} %copy-done.1), custom_call_target="tpu_custom_call" | custom-call | tf_op jit(solution)/shard_map/backward/pallas_call | solution.py:476
  80.5 0.0 copy-start
  80.5 0.8 %copy-done = f32[32,5,8,128]{3,2,1,0:T(8,128)} copy-done((f32[32,5,8,128]{3,2,1,0:T(8,128)}, f32[32,5,8,128]{3,2,1,0:T(8,128)S(1)}, u32[]{:S(2)}) %copy-start) | copy-done | bytes 655384
  81.4 2.2 %settle.1 = f32[160,4,256]{2,1,0:T(4,128)} custom-call(f32[32,5,8,128]{3,2,1,0:T(8,128)} %copy-done), custom_call_target="tpu_custom_call" | custom-call | tf_op jit(solution)/shard_map/settle/pallas_call | solution.py:621
  (4 shorter events, 0.0 us)
Async XLA Ops:
  0.0 0.7 copy-start.9
  0.7 0.7 copy-start.7
  0.7 0.7 copy-start.8
  1.4 1.1 %copy-start.3 = (f32[160,4,256]{2,1,0:T(4,128)S(1)}, f32[160,4,256]{2,1,0:T(4,128)}, u32[]{:S(2)}) copy-start(f32[160,4,256]{2,1,0:T(4,128)} %x_ref.1) | copy-start | bytes 1966084
  38.1 1.0 %copy-start.2 = (f32[3,128,640]{2,1,0:T(8,128)}, f32[3,128,640]{2,1,0:T(8,128)S(1)}, u32[]{:S(2)}) copy-start(f32[3,128,640]{2,1,0:T(8,128)S(1)} %get-tuple-element.11.yt_ref) | copy-start | bytes 2949124
  39.1 0.8 %copy-start.4 = (f32[256,640]{1,0:T(8,128)}, f32[256,640]{1,0:T(8,128)S(1)}, u32[]{:S(2)}) copy-start(f32[256,640]{1,0:T(8,128)S(1)} %get-tuple-element.9.at_ref) | copy-start | bytes 1966084
  39.9 0.6 copy-start.5
  40.6 0.6 copy-start.6
  59.5 1.1 %copy-start.1 = (f32[256,640]{1,0:T(8,128)S(1)}, f32[256,640]{1,0:T(8,128)}, u32[]{:S(2)}) copy-start(f32[256,640]{1,0:T(8,128)} %analysis.1.y_ref) | copy-start | bytes 1966084
  80.5 0.8 %copy-start = (f32[32,5,8,128]{3,2,1,0:T(8,128)}, f32[32,5,8,128]{3,2,1,0:T(8,128)S(1)}, u32[]{:S(2)}) copy-start(f32[32,5,8,128]{3,2,1,0:T(8,128)S(1)} %backward.1.z_ref) | copy-start | bytes 1966084

commit v3 on v0

v3 whole, which is shorter than its diff:
```python
import functools

import jax
import jax.numpy as jnp
from jax import lax
from jax.experimental import pallas as pl
from jax.experimental.pallas import tpu as pltpu
from jax.sharding import PartitionSpec as P

STEPS = 4

lat_coeff = 0.4
lon_coeff = 0.05
advect_coeff = 0.1

MESH = pl.DeviceIdType.MESH
LANES = 128


def with_halo(value, sides, width, wrap):
    for axis, dim in sides:
        size, length = (lax.axis_size(axis), value.shape[dim])
        up = [(i, (i + 1) % size) for i in range(size if wrap else size - 1)]
        down = [(j, i) for i, j in up]
        last = lax.slice_in_dim(value, length - width, length, axis=dim)
        initial = lax.slice_in_dim(value, 0, width, axis=dim)
        before = lax.ppermute(last, axis, up)
        after = lax.ppermute(initial, axis, down)
        value = jnp.concatenate([before, value, after], axis=dim)
    return value


def advance(padded):
    centre = padded[:, 1:-1]
    northern = padded[:, :-2]
    southern = padded[:, 2:]
    eastern = jnp.roll(centre, -1, axis=2)
    western = jnp.roll(centre, 1, axis=2)
    return (
        centre
        + lat_coeff * (northern + southern - 2.0 * centre)
        + lon_coeff * (eastern + western - 2.0 * centre)
        - advect_coeff * centre * (eastern - western)
    )


def localize(obs_rows, rel_cols, first_row, row_count, lat_scale, width_cols):
    lower = first_row.astype(jnp.float32)
    upper = lower + row_count.astype(jnp.float32) - 1.0
    lat_gap = jnp.maximum(jnp.maximum(lower - obs_rows, obs_rows - upper), 0.0) / lat_scale
    lon_gap = jnp.maximum(jnp.maximum(-rel_cols, rel_cols - (width_cols - 1.0)), 0.0) / width_cols
    return jnp.exp(-lat_gap * lat_gap - lon_gap * lon_gap)


def dot3(left, right):
    return jnp.matmul(left, right, precision=lax.Precision.HIGH, preferred_element_type=jnp.float32)


def analyse(anomaly, state_mean, spread, obs_meta, lengths, width_cols):
    cell_total, members = anomaly.shape
    lat_total = cell_total // width_cols
    near = spread.shape[0]
    starts = jnp.cumsum(lengths) - lengths
    cell_rows = jnp.arange(cell_total, dtype=jnp.int32) // width_cols
    identity = jnp.eye(members, dtype=jnp.float32)
    products = dot3(spread, jnp.concatenate([spread, anomaly], axis=0).T)
    common, crossed = products[:, :near], products[:, near:]
    innov = obs_meta[0]
    shrink = jnp.zeros((cell_total,), jnp.float32)
    shift = state_mean
    weights_all = jnp.zeros((near, cell_total), jnp.float32)
    for patch in range(lengths.shape[0]):
        weights = (
            localize(obs_meta[2], obs_meta[3], starts[patch], lengths[patch], lat_total / 4.0, float(width_cols))
            / obs_meta[1]
        )
        scale = jnp.sqrt(weights)
        gram_matrix = (members - 1.0) * identity + jnp.dot(
            (spread * weights[:, None]).T, spread, preferred_element_type=jnp.float32
        )
        bound = jnp.max(jnp.sum(jnp.abs(gram_matrix), axis=1))
        alpha = (members - 1.0) / bound
        x = common * scale[:, None] * (scale / bound)[None, :]
        c0 = 2.25 + alpha * (-2.4375 + alpha * (1.6875 + alpha * (-0.5625 + alpha * 0.0625)))
        c1 = -2.4375 + alpha * (3.375 + alpha * (-1.6875 + alpha * 0.25))
        c2 = 1.6875 + alpha * (-1.6875 + alpha * 0.375)
        c3 = -0.5625 + alpha * 0.25
        c4 = 0.0625
        x2 = dot3(x, x)
        x34 = dot3(x2, jnp.concatenate([x, x2], axis=1))
        x3, x4 = x34[:, :near], x34[:, near:]
        low = c2 * x + c3 * x2 + c4 * x3
        high = c1 * x + c2 * x2 + c3 * x3 + c4 * x4
        block = jnp.concatenate([crossed * scale[:, None], (scale * innov)[:, None]], axis=1)
        both = dot3(jnp.concatenate([low, high], axis=0), block)
        b1 = c1 * block + both[:near]
        b2 = c0 * block + both[near:]
        b3 = c0 * b2 + dot3(high, b2)
        mixed = alpha * c0 * b1 + b3
        got = 1.5 * b1 - 0.5 * (
            alpha * c0 * c0 * b1
            + c0 * mixed
            + dot3(high, mixed)
            + alpha * (c1 * b3 + dot3(low, b3))
        )
        base = c0 * (1.5 - 0.5 * alpha * c0 * c0)
        driven = base * block[:, -1] + jnp.sum(x * got[:, -1][None, :], axis=1)
        again = jnp.sum(x * driven[None, :], axis=1)
        mean_part = (
            jnp.sum(block[:, :-1] * (base * driven)[:, None] + got[:, :-1] * again[:, None], axis=0)
            / bound
        )
        cell_mask = (cell_rows >= starts[patch]) & (cell_rows < starts[patch] + lengths[patch])
        root_scale = jnp.sqrt((members - 1.0) / bound)
        shift = shift + jnp.where(cell_mask, mean_part, 0.0)
        shrink = jnp.where(cell_mask, root_scale * base, shrink)
        weights_all = jnp.where(
            cell_mask[None, :], got[:, :-1] * (scale * (root_scale / bound))[:, None], weights_all
        )
    return shift[:, None] + shrink[:, None] * anomaly + dot3(weights_all.T, spread)


def general_device(ensemble, obs_cell, obs_value, obs_var, patch_rows):
    members_dev, lat_rows, lon_cells = ensemble.shape
    lat_count = lax.axis_size("lat")
    member_count = lax.axis_size("member")
    servers = lat_count * member_count
    width_cols = lon_cells // servers
    padded = with_halo(ensemble, (("lat", 1),), STEPS, False)
    global_rows = (
        lax.axis_index("lat") * lat_rows + jnp.arange(lat_rows + 2 * STEPS, dtype=jnp.int32) - STEPS
    )
    inside = ((global_rows >= 0) & (global_rows < lat_rows * lat_count)).astype(jnp.float32)
    for step_index in range(STEPS):
        padded = advance(padded)
        keeper = inside[step_index + 1 : inside.shape[0] - step_index - 1]
        padded = padded * keeper[None, :, None]
    blocks = padded.reshape(1, members_dev, lat_rows, lon_cells)
    received = lax.all_to_all(blocks, ("member", "lat"), split_axis=3, concat_axis=0, tiled=True)
    strip = received.reshape(member_count, lat_count, members_dev, lat_rows, width_cols)
    members = member_count * members_dev
    lat_total = lat_count * lat_rows
    states = strip.transpose(1, 3, 4, 0, 2).reshape(lat_total * width_cols, members)
    cell_index = obs_cell[0]
    obs_count = cell_index.shape[0]
    state_mean = jnp.mean(states, axis=1)
    anomaly = states - state_mean[:, None]
    spread = jnp.take(anomaly, cell_index, axis=0)
    innov = obs_value[0] - jnp.take(state_mean, cell_index)
    obs_meta = jnp.stack(
        [
            innov,
            obs_var[0],
            (cell_index // width_cols).astype(jnp.float32),
            (cell_index % width_cols).astype(jnp.float32),
        ]
    )
    near_spread = with_halo(spread, ((("member", "lat"), 0),), obs_count, True)
    near_meta = with_halo(obs_meta, ((("member", "lat"), 1),), obs_count, True)
    shifts = jnp.repeat(jnp.array([-1.0, 0.0, 1.0], jnp.float32), obs_count) * width_cols
    near_meta = jnp.concatenate([near_meta[:3], (near_meta[3] + shifts)[None, :]], axis=0)
    analysed = analyse(anomaly, state_mean, near_spread, near_meta, patch_rows[0], width_cols)
    outgoing = analysed.reshape(lat_count, lat_rows, width_cols, member_count, members_dev)
    outgoing = outgoing.transpose(3, 0, 4, 1, 2).reshape(servers, members_dev, lat_rows, width_cols)
    returned = lax.all_to_all(outgoing, ("member", "lat"), split_axis=0, concat_axis=3, tiled=True)
    return returned.reshape(members_dev, lat_rows, lon_cells)


def place(block, lats):
    half = block // (lats // 2)
    return (1 - half) * (2 * block) + half * (2 * lats - 1 - 2 * block)


def block_at(lat, lats):
    odd = lat % 2
    return (1 - odd) * (lat // 2) + odd * (lats - 1 - lat // 2)


def member_of(block, q, members):
    odd = block % 2
    return (1 - odd) * q + odd * (members - 1 - q)


def strip_at(m, lat, lats, members):
    block = block_at(lat, lats)
    return block * members + member_of(block, m, members)


def home_of(strip, lats, members):
    block = strip // members
    return member_of(block, strip % members, members), place(block, lats)


def greet_all(lats, members):
    m, lat = lax.axis_index("member"), lax.axis_index("lat")
    barrier = pltpu.get_barrier_semaphore()
    for dm in range(members):
        for dl in range(lats):
            if dm == 0 and dl == 0:
                continue
            pl.semaphore_signal(
                barrier, inc=1, device_id=((m + dm) % members, (lat + dl) % lats), device_id_type=MESH
            )
    return barrier, lats * members - 1


def split(a):
    high = a.astype(jnp.bfloat16)
    return high, (a - high.astype(jnp.float32)).astype(jnp.bfloat16)


def dot_pairs(a, b, dims=(((1,), (0,)), ((), ()))):
    (ah, al), (bh, bl) = a, b
    one = functools.partial(lax.dot_general, dimension_numbers=dims, preferred_element_type=jnp.float32)
    return one(ah, bh) + (one(ah, bl) + one(al, bh))


def to_column(row):
    eye = lax.broadcasted_iota(jnp.int32, (LANES, LANES), 0) == lax.broadcasted_iota(jnp.int32, (LANES, LANES), 1)
    return jnp.concatenate(
        [
            jnp.sum(jnp.where(eye, row[:, i : i + LANES], 0.0), axis=1, keepdims=True)
            for i in range(0, row.shape[1], LANES)
        ],
        axis=0,
    )


def analysis(dims, at, mean, yt, y_mean, meta):
    lats, members, chunks, rows, width, group = dims
    cells, count = at.shape
    near = yt.shape[0]
    side = near // 3
    lat_total = cells // width
    y_pair = split(yt)
    a_pair = split(at)
    across = (((1,), (1,)), ((), ()))
    common = dot_pairs(y_pair, y_pair, across)
    crossed = dot_pairs(y_pair, a_pair, across)
    y_turned = yt.T

    strip_of = lax.broadcasted_iota(jnp.int32, (1, near), 1) // side - 1
    innov = to_column(meta[0:1]) - y_mean
    var, obs_rows = meta[1:2], meta[2:3]
    cols = meta[3:4] + (strip_of * width).astype(jnp.float32)
    lengths = [meta[4:5, side + i : side + i + 1] for i in range(2)]
    starts = [jnp.zeros_like(lengths[0]), lengths[0]]
    lon_gap = jnp.maximum(jnp.maximum(-cols, cols - (width - 1.0)), 0.0) / float(width)
    cell_row_lane = (lax.broadcasted_iota(jnp.int32, (1, cells), 1) // width).astype(jnp.float32)
    cell_row_col = (lax.broadcasted_iota(jnp.int32, (cells, 1), 0) // width).astype(jnp.float32)
    lane = lax.broadcasted_iota(jnp.int32, (near, cells), 1)

    shift = jnp.zeros((1, cells), jnp.float32)
    shrink = jnp.zeros((cells, 1), jnp.float32)
    combined = None
    for patch in range(2):
        lower = starts[patch]
        upper = lower + lengths[patch] - 1.0
        lat_gap = jnp.maximum(jnp.maximum(lower - obs_rows, obs_rows - upper), 0.0) / (lat_total / 4.0)
        weights = jnp.exp(-lat_gap * lat_gap - lon_gap * lon_gap) / var
        scale = jnp.sqrt(weights)
        left = (y_turned * weights).astype(jnp.bfloat16)
        sums = None
        for i in range(0, count, LANES):
            tile = jnp.abs(jnp.dot(left[i : i + LANES], y_pair[0], preferred_element_type=jnp.float32))
            part = jnp.sum(tile, axis=0, keepdims=True)
            sums = part if sums is None else sums + part
        bound = (count - 1.0) + jnp.max(sums, axis=1, keepdims=True)
        inverse = 1.0 / bound
        alpha = (count - 1.0) * inverse
        scale_col = to_column(scale)
        x = common * scale_col * (scale * inverse)
        c0 = 2.25 + alpha * (-2.4375 + alpha * (1.6875 + alpha * (-0.5625 + alpha * 0.0625)))
        c1 = -2.4375 + alpha * (3.375 + alpha * (-1.6875 + alpha * 0.25))
        c2 = 1.6875 + alpha * (-1.6875 + alpha * 0.375)
        c3 = -0.5625 + alpha * 0.25
        c4 = 0.0625
        x_pair = split(x)
        x2 = dot_pairs(x_pair, x_pair)
        low = c2 * x + c3 * x2 + c4 * dot_pairs(split(x2), x_pair)
        low_pair = split(low)
        spare = cells - 1 if patch == 0 else 0
        block = jnp.where(lane == spare, innov, crossed) * scale_col
        b_pair = split(block)
        b1 = c1 * block + dot_pairs(low_pair, b_pair)
        b2 = c0 * block + dot_pairs(x_pair, split(b1))
        w = c1 * b2 + dot_pairs(low_pair, split(b2))
        b3 = c0 * b2 + dot_pairs(x_pair, split(w))
        u = c1 * b3 + dot_pairs(low_pair, split(b3))
        z = c0 * b3 + dot_pairs(x_pair, split(u))
        got = 1.5 * b1 - 0.5 * (z + alpha * (u + c0 * (w + c0 * b1)))
        base = c0 * (1.5 - 0.5 * alpha * c0 * c0)
        full = base * block + dot_pairs(x_pair, split(got))
        drive = full[:, spare : spare + 1]
        mean_part = jnp.sum(full * drive, axis=0, keepdims=True) * inverse
        root_scale = jnp.sqrt(alpha)
        inside = jnp.logical_and(cell_row_lane >= lower, cell_row_lane <= upper)
        inside_col = jnp.logical_and(cell_row_col >= lower, cell_row_col <= upper)
        shift = jnp.where(inside, mean_part, shift)
        shrink = jnp.where(inside_col, root_scale * base, shrink)
        weighted = got * (scale_col * (root_scale * inverse))
        combined = weighted if combined is None else jnp.where(inside, weighted, combined)
    return (mean + to_column(shift)) + shrink * at + dot_pairs(split(combined.T), y_pair)


def forecast(load, lats, group):
    fields = [load(l) for l in range(lats)]
    lane = lax.broadcasted_iota(jnp.int32, fields[0].shape, 1)
    first, last = lane < group, lane >= LANES - group
    count = fields[0].shape[0]
    zero = jnp.zeros_like(fields[0])
    for _ in range(STEPS):
        new = []
        for l in range(lats):
            c = fields[l]
            above = fields[l - 1] if l > 0 else zero
            below = fields[l + 1] if l + 1 < lats else zero
            north = pltpu.roll(jnp.where(last, above, c), group, 1)
            south = pltpu.roll(jnp.where(first, below, c), LANES - group, 1)
            east = pltpu.roll(c, count - 1, 0)
            west = pltpu.roll(c, 1, 0)
            new.append(
                c
                + lat_coeff * (north + south - 2.0 * c)
                + lon_coeff * (east + west - 2.0 * c)
                - advect_coeff * c * (east - west)
            )
        fields = new
    return fields


def swap_blocks(parts, group):
    per = len(parts)
    lane_block = lax.broadcasted_iota(jnp.int32, parts[0].shape, 1) // group
    outs = []
    for i in range(per):
        out = None
        for j in range(per):
            shift = (group * (j - i)) % LANES
            piece = pltpu.roll(parts[j], shift, 1) if shift else parts[j]
            out = piece if out is None else jnp.where(lane_block == j, piece, out)
        outs.append(out)
    return outs


def pick(onehot, values):
    total, rest = None, values
    for _ in range(3):
        term = rest.astype(jnp.bfloat16)
        part = jnp.dot(onehot, term, preferred_element_type=jnp.float32)
        total = part if total is None else total + part
        rest = rest - term.astype(jnp.float32)
    return total


def engine_kernel(
    dims, x_hbm, cell_ref, value_ref, var_ref, rows_ref, z_hbm,
    x_buf, s_buf, ra, f_buf, r_buf, xt, yt, meta, obs_out, obs_in, t_buf,
    x_sem, a_send, a_recv, b_send, b_recv, o_send, o_recv, m_send, m_recv, y_send, y_recv, z_send, z_recv, own_sem,
):
    lats, members, chunks, rows, width, group = dims
    cols = width * members
    cells = lats * rows * width
    strips = lats * members
    edge = STEPS
    m, lat = lax.axis_index("member"), lax.axis_index("lat")
    own = block_at(lat, lats)
    strip = strip_at(m, lat, lats, members)
    neighbours = [(slot, home_of((strip + side) % strips, lats, members)) for side, slot in ((1, 0), (strips - 1, 2))]

    def remote(src, dst, send, recv, to):
        return pltpu.make_async_remote_copy(
            src_ref=src, dst_ref=dst, send_sem=send, recv_sem=recv, device_id=to, device_id_type=MESH
        )

    reads = [
        pltpu.make_async_copy(x_hbm.at[pl.ds(kc * group, group)], x_buf.at[kc], x_sem.at[kc]) for kc in range(chunks)
    ]
    for read in reads:
        read.start()
    barrier, partners = greet_all(lats, members)

    obs_out[...] = jnp.zeros_like(obs_out)
    obs_out[0:1, :] = cell_ref[...].astype(jnp.float32)
    obs_out[1:2, :] = value_ref[...]
    obs_out[2:3, :] = var_ref[...]
    obs_out[3:4, 0 : rows_ref.shape[1]] = rows_ref[...].astype(jnp.float32)

    target_m, target_l = home_of(m * lats + lat, lats, members)
    away = jnp.logical_or(target_m != m, target_l != lat)
    obs_copy = remote(obs_out, obs_in, o_send, o_recv, (target_m, target_l))

    a_copies = []
    for kc in range(chunks):
        reads[kc].wait()
        whole = jnp.concatenate([x_buf[kc, :, r, :] for r in range(rows)], axis=0)
        turned = whole.T
        lon = turned.shape[0]
        for b in range(lats):
            s_buf[kc, b, 0:cols] = turned[b * cols : (b + 1) * cols]
            east, west = ((b + 1) * cols) % lon, (b * cols - edge) % lon
            s_buf[kc, b, cols : cols + edge] = turned[east : east + edge]
            s_buf[kc, b, cols + edge : cols + 2 * edge] = turned[west : west + edge]
        if kc == 0:
            pl.semaphore_wait(barrier, partners)

            @pl.when(away)
            def _():
                obs_copy.start()

            @pl.when(jnp.logical_not(away))
            def _():
                obs_in[...] = obs_out[...]

        run = []
        for d in range(1, lats):
            to = (lat + d) % lats
            copy = remote(
                s_buf.at[kc, block_at(to, lats)], ra.at[kc, lat], a_send.at[kc, d], a_recv.at[kc, d], (m, to)
            )
            copy.start()
            run.append(copy)
        a_copies.append(run)

    @pl.when(away)
    def _():
        obs_copy.wait_recv()

    cell_lane = obs_in[0:1, :]
    obs_row = jnp.floor(cell_lane * (1.0 / width))
    meta[1, 0:1, :] = obs_in[1:2, :]
    meta[1, 1:2, :] = obs_in[2:3, :]
    meta[1, 2:3, :] = obs_row
    meta[1, 3:4, :] = cell_lane - width * obs_row
    meta[1, 4:5, :] = obs_in[3:4, :]
    meta[1, 5:8, :] = jnp.zeros((3, cell_lane.shape[1]), jnp.float32)
    late = []
    for slot, to in neighbours:
        copy = remote(meta.at[1], meta.at[slot], m_send.at[slot], m_recv.at[slot], to)
        copy.start()
        late.append(copy)
    onehot = (
        to_column(cell_lane)
        == lax.broadcasted_iota(jnp.int32, (cell_lane.shape[1], cells), 1).astype(jnp.float32)
    ).astype(jnp.bfloat16)

    b_copies = []

    def arrive(kc):
        for copy in b_copies[kc]:
            copy.wait_recv()
        parts = [r_buf[j, kc].reshape(lats * width, LANES) for j in range(members)]
        for r, out in enumerate(swap_blocks(parts, group)):
            for l in range(lats):
                xt[kc, (l * rows + r) * width : (l * rows + r + 1) * width] = out[l * width : (l + 1) * width]
        yt[1, kc] = pick(onehot, xt[kc])
        for slot, to in neighbours:
            copy = remote(yt.at[1, kc], yt.at[slot, kc], y_send.at[slot, kc], y_recv.at[slot, kc], to)
            copy.start()
            late.append(copy)

    for kc in range(chunks):
        ra[kc, lat] = s_buf[kc, own]
        for copy in a_copies[kc]:
            copy.wait_recv()
        fields = forecast(lambda l, kc=kc: ra[kc, l], lats, group)
        for l in range(lats):
            for q in range(members):
                f_buf[kc, q, l] = fields[l][q * width : (q + 1) * width]
        run = []
        for d in range(1, members):
            to = (m + d) % members
            copy = remote(
                f_buf.at[kc, member_of(own, to, members)], r_buf.at[m, kc], b_send.at[kc, d], b_recv.at[kc, d], (to, lat)
            )
            copy.start()
            run.append(copy)
        b_copies.append(run)
        r_buf[m, kc] = f_buf[kc, member_of(own, m, members)]
        if kc:
            arrive(kc - 1)
    arrive(chunks - 1)

    states = jnp.concatenate([xt[kc] for kc in range(chunks)], axis=1)
    mean = jnp.sum(states, axis=1, keepdims=True) * (1.0 / states.shape[1])
    at = states - mean
    for copy in late:
        copy.wait_recv()
    y_raw = jnp.concatenate(
        [jnp.concatenate([yt[slot, kc] for kc in range(chunks)], axis=1) for slot in range(3)], axis=0
    )
    y_mean = jnp.sum(y_raw, axis=1, keepdims=True) * (1.0 / y_raw.shape[1])
    all_meta = jnp.concatenate([meta[slot] for slot in range(3)], axis=1)
    analysed = analysis(dims, at, mean, y_raw - y_mean, y_mean, all_meta)

    for kc in range(chunks):
        lanes = analysed[:, kc * LANES : (kc + 1) * LANES]
        parts = [
            jnp.concatenate(
                [lanes[(l * rows + r) * width : (l * rows + r + 1) * width] for l in range(lats)], axis=0
            )
            for r in range(rows)
        ]
        for j, out in enumerate(swap_blocks(parts, group)):
            for l in range(lats):
                t_buf[j, l, kc] = out[l * width : (l + 1) * width]
    z_copies = []
    for dl in range(lats):
        for dm in range(members):
            if dm == 0 and dl == 0:
                continue
            to = ((m + dm) % members, (lat + dl) % lats)
            copy = remote(t_buf.at[to[0], to[1]], z_hbm.at[strip], z_send.at[dl, dm], z_recv.at[dl, dm], to)
            copy.start()
            z_copies.append(copy)
    kept = pltpu.make_async_copy(t_buf.at[m, lat], z_hbm.at[strip], own_sem)
    kept.start()

    for run in a_copies + b_copies + [late]:
        for copy in run:
            copy.wait_send()

    @pl.when(away)
    def _():
        obs_copy.wait_send()

    kept.wait()
    for copy in z_copies:
        copy.wait()


def engine(ensemble, obs_cell, obs_value, obs_var, patch_rows, dims):
    lats, members, chunks, rows, width, group = dims
    cells = lats * rows * width
    nobs = obs_cell.shape[1]
    strips = lats * members
    dma, f32 = pltpu.SemaphoreType.DMA, jnp.float32
    vmem, anywhere = pl.BlockSpec(memory_space=pltpu.VMEM), pl.BlockSpec(memory_space=pl.ANY)
    block = (chunks, lats, members * width + 2 * STEPS, LANES)
    return pl.pallas_call(
        functools.partial(engine_kernel, dims),
        out_shape=jax.ShapeDtypeStruct((strips, chunks, width, LANES), f32),
        in_specs=[anywhere, vmem, vmem, vmem, vmem],
        out_specs=anywhere,
        scratch_shapes=[
            pltpu.VMEM((chunks, group, rows, strips * width), f32),
            pltpu.VMEM(block, f32),
            pltpu.VMEM(block, f32),
            pltpu.VMEM((chunks, members, lats, width, LANES), f32),
            pltpu.VMEM((members, chunks, lats, width, LANES), f32),
            pltpu.VMEM((chunks, cells, LANES), f32),
            pltpu.VMEM((3, chunks, nobs, LANES), f32),
            pltpu.VMEM((3, 8, nobs), f32),
            pltpu.VMEM((8, nobs), f32),
            pltpu.VMEM((8, nobs), f32),
            pltpu.VMEM((members, lats, chunks, width, LANES), f32),
            dma((chunks,)),
            dma((chunks, lats)),
            dma((chunks, lats)),
            dma((chunks, members)),
            dma((chunks, members)),
            dma,
            dma,
            dma((3,)),
            dma((3,)),
            dma((3, chunks)),
            dma((3, chunks)),
            dma((lats, members)),
            dma((lats, members)),
            dma,
        ],
        compiler_params=pltpu.CompilerParams(
            collective_id=0, has_side_effects=True, vmem_limit_bytes=56 * 1024 * 1024
        ),
        name="engine",
    )(ensemble, obs_cell, obs_value, obs_var, patch_rows)


def settle_kernel(dims, z_ref, out_ref):
    lats, members, chunks, rows, width, group = dims
    turned = z_ref[...].reshape(lats * members * width, LANES).T
    for r in range(rows):
        out_ref[:, r, :] = turned[r * group : (r + 1) * group]


def settle(pieces, dims):
    lats, members, chunks, rows, width, group = dims
    strips = lats * members
    return pl.pallas_call(
        functools.partial(settle_kernel, dims),
        grid=(chunks,),
        out_shape=jax.ShapeDtypeStruct((chunks * group, rows, strips * width), jnp.float32),
        in_specs=[pl.BlockSpec((strips, None, width, LANES), lambda kc: (0, kc, 0, 0))],
        out_specs=pl.BlockSpec((group, rows, strips * width), lambda kc: (kc, 0, 0)),
        name="settle",
    )(pieces)


def kernel_device(dims, ensemble, obs_cell, obs_value, obs_var, patch_rows):
    return settle(engine(ensemble, obs_cell, obs_value, obs_var, patch_rows, dims), dims)


def kernel_dims(mesh, ensemble, obs_cell, patch_rows):
    lats, members = mesh.shape["lat"], mesh.shape["member"]
    total, lat_all, lon = ensemble.shape
    own, rows = total // members, lat_all // lats
    width = lon // (lats * members)
    if LANES % rows:
        return None
    group = LANES // rows
    fits = (
        own % group == 0
        and (members * (own // group)) % rows == 0
        and width == 8
        and lats % 2 == 0
        and members % 2 == 0
        and obs_cell.shape[1] % LANES == 0
        and patch_rows.shape[1] == 2
    )
    return (lats, members, own // group, rows, width, group) if fits else None


def solution(mesh):
    specs = (P("member", "lat", None),) + (P(("member", "lat"), None),) * 4

    def run(ensemble, obs_cell, obs_value, obs_var, patch_rows):
        dims = kernel_dims(mesh, ensemble, obs_cell, patch_rows)
        body = general_device if dims is None else functools.partial(kernel_device, dims)
        mapped = jax.shard_map(
            body, mesh=mesh, in_specs=specs, out_specs=P("member", "lat", None), check_vma=False
        )
        return mapped(ensemble, obs_cell, obs_value, obs_var, patch_rows)

    return run
```

time: 165 us -> 70.8 us (0.43)
  the two profiles are of different devices: /device:TPU:0 before, /device:TPU:11 now
where the time goes in v3:
time: 70.8 us; the launch traced here: 70.6 us
  Pallas kernels  70.6 us (100%)
    pallas_call x1, Pallas kernels, engine(): pl.pallas_call(functools.partial(engine_kernel, dims), out_shape=jax.Shap...  66.7 us
    pallas_call x1, Pallas kernels, settle(): pl.pallas_call(functools.partial(settle_kernel, dims), grid=(chunks,), ou...  3.83 us

profile of v3, /device:TPU:11, one launch (start us, length us, event | category | flops | bytes accessed | tf_op | source)
XLA Modules:
  0.0 70.6 jit_solution(9553688156540990491)
XLA Ops:
  0.0 66.7 %engine.1.z_ref = f32[32,5,8,128]{3,2,1,0:T(8,128)} custom-call(f32[160,4,256]{2,1,0:T(4,128)} %x_hbm.1, s32[1,128]{1,0:T(1,128)} %cell_ref.1, f32[1,128]{1,0:T(1,128)} %value_ref.1, f32[1,128]{1,0:T(1,128)} %var_ref.1, s32[1,2]{1,0:T(1,128)} %rows_ref.1), custom_call_target="tpu_custom_call" | custom-call | tf_op jit(solution)/shard_map/engine/pallas_call | solution.py:540
  66.8 3.8 %settle.1 = f32[160,4,256]{2,1,0:T(4,128)} custom-call(f32[32,5,8,128]{3,2,1,0:T(8,128)} %engine.1.z_ref), custom_call_target="tpu_custom_call" | custom-call | tf_op jit(solution)/shard_map/settle/pallas_call | solution.py:589

commit v4 on v3

--- a/solution.py
+++ b/solution.py
@@ -209,10 +209,26 @@
     return high, (a - high.astype(jnp.float32)).astype(jnp.bfloat16)
 
 
-def dot_pairs(a, b, dims=(((1,), (0,)), ((), ()))):
-    (ah, al), (bh, bl) = a, b
-    one = functools.partial(lax.dot_general, dimension_numbers=dims, preferred_element_type=jnp.float32)
-    return one(ah, bh) + (one(ah, bl) + one(al, bh))
+def left_form(a):
+    high, low = split(a)
+    return jnp.concatenate([high, high, low], axis=1)
+
+
+def put_right(ref, at, a):
+    high, low = split(a)
+    depth = ref.shape[0] // 3
+    rows = a.shape[0]
+    ref[at : at + rows] = high
+    ref[depth + at : depth + at + rows] = low
+    ref[2 * depth + at : 2 * depth + at + rows] = high
+
+
+def dot(a, b):
+    return jnp.dot(a, b, preferred_element_type=jnp.float32)
+
+
+def dot_across(a, b):
+    return lax.dot_general(a, b, (((1,), (1,)), ((), ())), preferred_element_type=jnp.float32)
 
 
 def to_column(row):
@@ -226,81 +242,120 @@
     )
 
 
-def analysis(dims, at, mean, yt, y_mean, meta):
+def analysis_scratch(cells, count, near):
+    f32, bf16 = jnp.float32, jnp.bfloat16
+    return [
+        pltpu.VMEM((near, near), f32),
+        pltpu.VMEM((near, cells), f32),
+        pltpu.VMEM((3 * near, count), bf16),
+        pltpu.VMEM((count, near), bf16),
+        pltpu.VMEM((near, 3 * near), bf16),
+        pltpu.VMEM((3 * near, near), bf16),
+        pltpu.VMEM((near, 3 * near), bf16),
+        pltpu.VMEM((8, 3 * near, cells), bf16),
+        pltpu.VMEM((7, near, cells), f32),
+        pltpu.VMEM((2, cells, near), f32),
+    ]
+
+
+def products(work, y, at):
+    common, crossed, y_right, y_turned = work[:4]
+    near = y.shape[0]
+    put_right(y_right, 0, y)
+    yh, yl = y_right[0:near], y_right[near : 2 * near]
+    ah, al = split(at)
+    y_turned[...] = yh.T
+    right = jnp.concatenate([yh, ah], axis=0)
+    right = jnp.concatenate([right, jnp.concatenate([yl, al], axis=0), right], axis=1)
+    both = dot_across(jnp.concatenate([yh, yh, yl], axis=1), right)
+    common[...] = both[:, :near]
+    crossed[...] = both[:, near:]
+
+
+def solve_patch(dims, work, slot, spare_first, lower, upper, innov, meta):
     lats, members, chunks, rows, width, group = dims
-    cells, count = at.shape
-    near = yt.shape[0]
-    side = near // 3
-    lat_total = cells // width
-    y_pair = split(yt)
-    a_pair = split(at)
-    across = (((1,), (1,)), ((), ()))
-    common = dot_pairs(y_pair, y_pair, across)
-    crossed = dot_pairs(y_pair, a_pair, across)
-    y_turned = yt.T
-
-    strip_of = lax.broadcasted_iota(jnp.int32, (1, near), 1) // side - 1
-    innov = to_column(meta[0:1]) - y_mean
+    common, crossed, y_right, y_turned, x_left, x_right, low_left, b_right, blocks, turned = work
+    count, near = y_turned.shape
+    cells = crossed.shape[1]
+    tile = near // 2
+    tiles = range(0, near, tile)
     var, obs_rows = meta[1:2], meta[2:3]
+    strip_of = lax.broadcasted_iota(jnp.int32, (1, near), 1) // (near // 3) - 1
     cols = meta[3:4] + (strip_of * width).astype(jnp.float32)
-    lengths = [meta[4:5, side + i : side + i + 1] for i in range(2)]
-    starts = [jnp.zeros_like(lengths[0]), lengths[0]]
     lon_gap = jnp.maximum(jnp.maximum(-cols, cols - (width - 1.0)), 0.0) / float(width)
-    cell_row_lane = (lax.broadcasted_iota(jnp.int32, (1, cells), 1) // width).astype(jnp.float32)
-    cell_row_col = (lax.broadcasted_iota(jnp.int32, (cells, 1), 0) // width).astype(jnp.float32)
-    lane = lax.broadcasted_iota(jnp.int32, (near, cells), 1)
-
-    shift = jnp.zeros((1, cells), jnp.float32)
-    shrink = jnp.zeros((cells, 1), jnp.float32)
-    combined = None
-    for patch in range(2):
-        lower = starts[patch]
-        upper = lower + lengths[patch] - 1.0
-        lat_gap = jnp.maximum(jnp.maximum(lower - obs_rows, obs_rows - upper), 0.0) / (lat_total / 4.0)
-        weights = jnp.exp(-lat_gap * lat_gap - lon_gap * lon_gap) / var
-        scale = jnp.sqrt(weights)
-        left = (y_turned * weights).astype(jnp.bfloat16)
-        sums = None
-        for i in range(0, count, LANES):
-            tile = jnp.abs(jnp.dot(left[i : i + LANES], y_pair[0], preferred_element_type=jnp.float32))
-            part = jnp.sum(tile, axis=0, keepdims=True)
-            sums = part if sums is None else sums + part
-        bound = (count - 1.0) + jnp.max(sums, axis=1, keepdims=True)
-        inverse = 1.0 / bound
-        alpha = (count - 1.0) * inverse
-        scale_col = to_column(scale)
-        x = common * scale_col * (scale * inverse)
-        c0 = 2.25 + alpha * (-2.4375 + alpha * (1.6875 + alpha * (-0.5625 + alpha * 0.0625)))
-        c1 = -2.4375 + alpha * (3.375 + alpha * (-1.6875 + alpha * 0.25))
-        c2 = 1.6875 + alpha * (-1.6875 + alpha * 0.375)
-        c3 = -0.5625 + alpha * 0.25
-        c4 = 0.0625
-        x_pair = split(x)
-        x2 = dot_pairs(x_pair, x_pair)
-        low = c2 * x + c3 * x2 + c4 * dot_pairs(split(x2), x_pair)
-        low_pair = split(low)
-        spare = cells - 1 if patch == 0 else 0
-        block = jnp.where(lane == spare, innov, crossed) * scale_col
-        b_pair = split(block)
-        b1 = c1 * block + dot_pairs(low_pair, b_pair)
-        b2 = c0 * block + dot_pairs(x_pair, split(b1))
-        w = c1 * b2 + dot_pairs(low_pair, split(b2))
-        b3 = c0 * b2 + dot_pairs(x_pair, split(w))
-        u = c1 * b3 + dot_pairs(low_pair, split(b3))
-        z = c0 * b3 + dot_pairs(x_pair, split(u))
-        got = 1.5 * b1 - 0.5 * (z + alpha * (u + c0 * (w + c0 * b1)))
-        base = c0 * (1.5 - 0.5 * alpha * c0 * c0)
-        full = base * block + dot_pairs(x_pair, split(got))
-        drive = full[:, spare : spare + 1]
-        mean_part = jnp.sum(full * drive, axis=0, keepdims=True) * inverse
-        root_scale = jnp.sqrt(alpha)
-        inside = jnp.logical_and(cell_row_lane >= lower, cell_row_lane <= upper)
-        inside_col = jnp.logical_and(cell_row_col >= lower, cell_row_col <= upper)
-        shift = jnp.where(inside, mean_part, shift)
-        shrink = jnp.where(inside_col, root_scale * base, shrink)
-        weighted = got * (scale_col * (root_scale * inverse))
-        combined = weighted if combined is None else jnp.where(inside, weighted, combined)
-    return (mean + to_column(shift)) + shrink * at + dot_pairs(split(combined.T), y_pair)
+    lat_gap = jnp.maximum(jnp.maximum(lower - obs_rows, obs_rows - upper), 0.0) / (cells // width / 4.0)
+    weights = jnp.exp(-lat_gap * lat_gap - lon_gap * lon_gap) / var
+    scale = jnp.sqrt(weights)
+    scale_col = to_column(scale)
+
+    left = (y_turned[...].astype(jnp.float32) * weights).astype(jnp.bfloat16)
+    gram = jnp.abs(dot(left, y_right[0:near]))
+    sums = jnp.sum(gram.reshape(count // 8, 8, count), axis=0)
+    bound = (count - 1.0) + jnp.max(jnp.sum(sums, axis=0, keepdims=True), axis=1, keepdims=True)
+    inverse = 1.0 / bound
+    alpha = (count - 1.0) * inverse
+    c0 = 2.25 + alpha * (-2.4375 + alpha * (1.6875 + alpha * (-0.5625 + alpha * 0.0625)))
+    c1 = -2.4375 + alpha * (3.375 + alpha * (-1.6875 + alpha * 0.25))
+    c2 = 1.6875 + alpha * (-1.6875 + alpha * 0.375)
+    c3 = -0.5625 + alpha * 0.25
+    c4 = 0.0625
+
+    lane = lax.broadcasted_iota(jnp.int32, (tile, cells), 1)
+    spare = (1 - spare_first) * (cells - 1)
+    scale_row = scale * inverse
+
+    def x_tile(i):
+        return common[i : i + tile] * scale_col[i : i + tile] * scale_row
+
+    block, b1, b2, w, b3, u, got = range(7)
+
+    def keep(i, which, value):
+        blocks[which, i : i + tile] = value
+        put_right(b_right.at[which], i, value)
+
+    for i in tiles:
+        x = x_tile(i)
+        x_left[i : i + tile] = left_form(x)
+        put_right(x_right, i, x)
+        keep(i, block, jnp.where(lane == spare, innov[i : i + tile], crossed[i : i + tile]) * scale_col[i : i + tile])
+    for i in tiles:
+        x2 = dot(x_left[i : i + tile], x_right[...])
+        x3 = dot(left_form(x2), x_right[...])
+        low_left[i : i + tile] = left_form(c2 * x_tile(i) + c3 * x2 + c4 * x3)
+
+    def low_on(i, which):
+        return dot(low_left[i : i + tile], b_right[which])
+
+    def x_on(i, which):
+        return dot(x_left[i : i + tile], b_right[which])
+
+    for i in tiles:
+        keep(i, b1, c1 * blocks[block, i : i + tile] + low_on(i, block))
+    for i in tiles:
+        keep(i, b2, c0 * blocks[block, i : i + tile] + x_on(i, b1))
+    for i in tiles:
+        keep(i, w, c1 * blocks[b2, i : i + tile] + low_on(i, b2))
+    for i in tiles:
+        keep(i, b3, c0 * blocks[b2, i : i + tile] + x_on(i, w))
+    for i in tiles:
+        keep(i, u, c1 * blocks[b3, i : i + tile] + low_on(i, b3))
+    root_scale = jnp.sqrt(alpha)
+    for i in tiles:
+        z = c0 * blocks[b3, i : i + tile] + x_on(i, u)
+        first = blocks[b1, i : i + tile]
+        value = 1.5 * first - 0.5 * (
+            z + alpha * (blocks[u, i : i + tile] + c0 * (blocks[w, i : i + tile] + c0 * first))
+        )
+        put_right(b_right.at[got], i, value)
+        turned[slot, :, i : i + tile] = (value * (scale_col[i : i + tile] * (root_scale * inverse))).T
+    base = c0 * (1.5 - 0.5 * alpha * c0 * c0)
+    change = None
+    for i in tiles:
+        full = base * blocks[block, i : i + tile] + x_on(i, got)
+        drive = jnp.where(spare_first == 1, full[:, 0:1], full[:, cells - 1 : cells])
+        part = jnp.sum((full * drive).reshape(tile // 8, 8, cells), axis=0)
+        change = part if change is None else change + part
+    return jnp.sum(change, axis=0, keepdims=True) * inverse, root_scale * base
 
 
 def forecast(load, lats, group):
@@ -355,8 +410,8 @@
 
 def engine_kernel(
     dims, x_hbm, cell_ref, value_ref, var_ref, rows_ref, z_hbm,
-    x_buf, s_buf, ra, f_buf, r_buf, xt, yt, meta, obs_out, obs_in, t_buf,
-    x_sem, a_send, a_recv, b_send, b_recv, o_send, o_recv, m_send, m_recv, y_send, y_recv, z_send, z_recv, own_sem,
+    x_buf, s_buf, ra, f_buf, r_buf, xt, yt, meta, obs_out, obs_in, t_buf, at_buf,
+    x_sem, a_send, a_recv, b_send, b_recv, o_send, o_recv, m_send, m_recv, y_send, y_recv, z_send, z_recv, own_sem, *work,
 ):
     lats, members, chunks, rows, width, group = dims
     cols = width * members
@@ -484,6 +539,7 @@
     states = jnp.concatenate([xt[kc] for kc in range(chunks)], axis=1)
     mean = jnp.sum(states, axis=1, keepdims=True) * (1.0 / states.shape[1])
     at = states - mean
+    at_buf[...] = at
     for copy in late:
         copy.wait_recv()
     y_raw = jnp.concatenate(
@@ -491,28 +547,77 @@
     )
     y_mean = jnp.sum(y_raw, axis=1, keepdims=True) * (1.0 / y_raw.shape[1])
     all_meta = jnp.concatenate([meta[slot] for slot in range(3)], axis=1)
-    analysed = analysis(dims, at, mean, y_raw - y_mean, y_mean, all_meta)
-
-    for kc in range(chunks):
-        lanes = analysed[:, kc * LANES : (kc + 1) * LANES]
-        parts = [
-            jnp.concatenate(
-                [lanes[(l * rows + r) * width : (l * rows + r + 1) * width] for l in range(lats)], axis=0
-            )
-            for r in range(rows)
-        ]
-        for j, out in enumerate(swap_blocks(parts, group)):
-            for l in range(lats):
-                t_buf[j, l, kc] = out[l * width : (l + 1) * width]
+    innov = to_column(all_meta[0:1]) - y_mean
+    products(work, y_raw - y_mean, at)
+    y_right, turned = work[2], work[9]
+
+    nobs = cell_lane.shape[1]
+    sure = lats // 4
+    rest = lats - sure
+    last = 1 - lat // (lats // 2)
+    lasts = last.astype(jnp.float32)
+    first_len = all_meta[4:5, nobs : nobs + 1]
+    second_len = all_meta[4:5, nobs + 1 : nobs + 2]
+    spans = []
+    for which in (lasts, 1.0 - lasts):
+        lower = which * first_len
+        spans.append((lower, lower + (first_len + which * (second_len - first_len)) - 1.0))
+
+    def finish(tile, tiles, pick_cells, weights, change, factor):
+        begin = tile * (rows * width)
+        span = pl.ds(pl.multiple_of(begin, rows * width), tiles * rows * width)
+        out = pick_cells(mean) + change + factor * at_buf[span, :] + dot(left_form(weights), y_right[...])
+        for kc in range(chunks):
+            lanes = out[:, kc * LANES : (kc + 1) * LANES]
+            parts = [
+                jnp.concatenate(
+                    [lanes[(l * rows + r) * width : (l * rows + r + 1) * width] for l in range(tiles)], axis=0
+                )
+                for r in range(rows)
+            ]
+            for j, piece in enumerate(swap_blocks(parts, group)):
+                for l in range(tiles):
+                    t_buf[j, tile + l, kc] = piece[l * width : (l + 1) * width]
+
+    def give(to):
+        copy = remote(t_buf.at[to[0], to[1]], z_hbm.at[strip], z_send.at[len(z_copies)], z_recv.at[strip], to)
+        copy.start()
+        z_copies.append(copy)
+
     z_copies = []
-    for dl in range(lats):
+    cut, tail = sure * rows * width, rest * rows * width
+    early = last * rest
+    change, factor = solve_patch(dims, work, 0, last, *spans[0], innov, all_meta)
+    change_col = to_column(change)
+
+    def far(column):
+        return jnp.where(last == 1, column[tail:], column[:cut])
+
+    def near(column):
+        return jnp.where(last == 1, column[:tail], column[cut:])
+
+    finish(early, sure, far, far(turned[0]), far(change_col), factor)
+    for l in range(sure):
         for dm in range(members):
-            if dm == 0 and dl == 0:
-                continue
-            to = ((m + dm) % members, (lat + dl) % lats)
-            copy = remote(t_buf.at[to[0], to[1]], z_hbm.at[strip], z_send.at[dl, dm], z_recv.at[dl, dm], to)
-            copy.start()
-            z_copies.append(copy)
+            give(((m + dm) % members, early + l))
+
+    change2, factor2 = solve_patch(dims, work, 1, 1 - last, *spans[1], innov, all_meta)
+    cell_row = (lax.broadcasted_iota(jnp.int32, (cells, 1), 0) // width).astype(jnp.float32)
+    inside = near(jnp.logical_and(cell_row >= spans[0][0], cell_row <= spans[0][1]).astype(jnp.float32)) > 0.5
+    base = (1 - last) * sure
+    finish(
+        base,
+        rest,
+        near,
+        jnp.where(inside, near(turned[0]), near(turned[1])),
+        jnp.where(inside, near(change_col), near(to_column(change2))),
+        jnp.where(inside, factor, factor2),
+    )
+    for j in range(rest - 1):
+        for dm in range(members):
+            give(((m + dm) % members, base + (lat - base + 1 + j) % rest))
+    for dm in range(1, members):
+        give(((m + dm) % members, lat))
     kept = pltpu.make_async_copy(t_buf.at[m, lat], z_hbm.at[strip], own_sem)
     kept.start()
 
@@ -526,7 +631,12 @@
 
     kept.wait()
     for copy in z_copies:
-        copy.wait()
+        copy.wait_send()
+    for d in range(1, strips):
+        other = (strip + d) % strips
+        remote(
+            t_buf.at[0, 0], z_hbm.at[other], z_send.at[0], z_recv.at[other], ((m + 1) % members, lat)
+        ).wait_recv()
 
 
 def engine(ensemble, obs_cell, obs_value, obs_var, patch_rows, dims):
@@ -554,6 +664,7 @@
             pltpu.VMEM((8, nobs), f32),
             pltpu.VMEM((8, nobs), f32),
             pltpu.VMEM((members, lats, chunks, width, LANES), f32),
+            pltpu.VMEM((cells, members * chunks * group), f32),
             dma((chunks,)),
             dma((chunks, lats)),
             dma((chunks, lats)),
@@ -565,10 +676,11 @@
             dma((3,)),
             dma((3, chunks)),
             dma((3, chunks)),
-            dma((lats, members)),
-            dma((lats, members)),
+            dma((strips,)),
+            dma((strips,)),
             dma,
-        ],
+        ]
+        + analysis_scratch(cells, members * chunks * group, 3 * nobs),
         compiler_params=pltpu.CompilerParams(
             collective_id=0, has_side_effects=True, vmem_limit_bytes=56 * 1024 * 1024
         ),
@@ -612,7 +724,7 @@
         own % group == 0
         and (members * (own // group)) % rows == 0
         and width == 8
-        and lats % 2 == 0
+        and lats % 4 == 0
         and members % 2 == 0
         and obs_cell.shape[1] % LANES == 0
         and patch_rows.shape[1] == 2

time: 70.8 us -> 62 us (0.88)
  Pallas kernels: 70.6 us -> 61.2 us
    pallas_call x1, Pallas kernels: 66.7 us -> 57.3 us  [engine(): pl.pallas_call(functools.partial(engine_kernel, dims), out_shape=jax.Shap...]
where the time goes in v4:
time: 62 us; the launch traced here: 61.2 us
  Pallas kernels  61.2 us (99%)
    pallas_call x1, Pallas kernels, engine(): pl.pallas_call(functools.partial(engine_kernel, dims), out_shape=jax.Shap...  57.3 us
    pallas_call x1, Pallas kernels, settle(): pl.pallas_call(functools.partial(settle_kernel, dims), grid=(chunks,), ou...  3.83 us

profile of v4, /device:TPU:11, one launch (start us, length us, event | category | flops | bytes accessed | tf_op | source)
XLA Modules:
  0.0 61.2 jit_solution(1245320928200557602)
XLA Ops:
  0.0 57.3 %engine.1.z_ref = f32[32,5,8,128]{3,2,1,0:T(8,128)} custom-call(f32[160,4,256]{2,1,0:T(4,128)} %x_hbm.1, s32[1,128]{1,0:T(1,128)} %cell_ref.1, f32[1,128]{1,0:T(1,128)} %value_ref.1, f32[1,128]{1,0:T(1,128)} %var_ref.1, s32[1,2]{1,0:T(1,128)} %rows_ref.1), custom_call_target="tpu_custom_call" | custom-call | tf_op jit(solution)/shard_map/engine/pallas_call | solution.py:650
  57.4 3.8 %settle.1 = f32[160,4,256]{2,1,0:T(4,128)} custom-call(f32[32,5,8,128]{3,2,1,0:T(8,128)} %engine.1.z_ref), custom_call_target="tpu_custom_call" | custom-call | tf_op jit(solution)/shard_map/settle/pallas_call | solution.py:701

commit v5 on v4

--- a/solution.py
+++ b/solution.py
@@ -688,22 +688,39 @@
     )(ensemble, obs_cell, obs_value, obs_var, patch_rows)
 
 
-def settle_kernel(dims, z_ref, out_ref):
+def settle_kernel(dims, z_hbm, out_hbm, z_buf, out_buf, in_sem, out_sem):
     lats, members, chunks, rows, width, group = dims
-    turned = z_ref[...].reshape(lats * members * width, LANES).T
-    for r in range(rows):
-        out_ref[:, r, :] = turned[r * group : (r + 1) * group]
+    reads = [pltpu.make_async_copy(z_hbm.at[:, kc], z_buf.at[kc], in_sem.at[kc]) for kc in range(chunks)]
+    for read in reads:
+        read.start()
+    writes = []
+    for kc in range(chunks):
+        reads[kc].wait()
+        turned = z_buf[kc].reshape(lats * members * width, LANES).T
+        for r in range(rows):
+            out_buf[kc, :, r, :] = turned[r * group : (r + 1) * group]
+        write = pltpu.make_async_copy(out_buf.at[kc], out_hbm.at[pl.ds(kc * group, group)], out_sem.at[kc])
+        write.start()
+        writes.append(write)
+    for write in writes:
+        write.wait()
 
 
 def settle(pieces, dims):
     lats, members, chunks, rows, width, group = dims
     strips = lats * members
+    f32, anywhere = jnp.float32, pl.BlockSpec(memory_space=pl.ANY)
     return pl.pallas_call(
         functools.partial(settle_kernel, dims),
-        grid=(chunks,),
-        out_shape=jax.ShapeDtypeStruct((chunks * group, rows, strips * width), jnp.float32),
-        in_specs=[pl.BlockSpec((strips, None, width, LANES), lambda kc: (0, kc, 0, 0))],
-        out_specs=pl.BlockSpec((group, rows, strips * width), lambda kc: (kc, 0, 0)),
+        out_shape=jax.ShapeDtypeStruct((chunks * group, rows, strips * width), f32),
+        in_specs=[anywhere],
+        out_specs=anywhere,
+        scratch_shapes=[
+            pltpu.VMEM((chunks, strips, width, LANES), f32),
+            pltpu.VMEM((chunks, group, rows, strips * width), f32),
+            pltpu.SemaphoreType.DMA((chunks,)),
+            pltpu.SemaphoreType.DMA((chunks,)),
+        ],
         name="settle",
     )(pieces)
 

time: 62 us -> 60.5 us (0.976)
  Pallas kernels: 61.2 us -> 59.5 us
    pallas_call x1, Pallas kernels: 3.83 us -> 2.2 us  [settle(): pl.pallas_call(functools.partial(settle_kernel, dims), out_shape=jax.Shap...]
where the time goes in v5:
time: 60.5 us; the launch traced here: 59.7 us
  Pallas kernels  59.5 us (98%)
    pallas_call x1, Pallas kernels, engine(): pl.pallas_call(functools.partial(engine_kernel, dims), out_shape=jax.Shap...  57.3 us
    pallas_call x1, Pallas kernels, settle(): pl.pallas_call(functools.partial(settle_kernel, dims), out_shape=jax.Shap...  2.2 us

profile of v5, /device:TPU:11, one launch (start us, length us, event | category | flops | bytes accessed | tf_op | source)
XLA Modules:
  0.0 59.7 jit_solution(10093268769077817078)
XLA Ops:
  0.0 57.3 %engine.1.z_hbm = f32[32,5,8,128]{3,2,1,0:T(8,128)} custom-call(f32[160,4,256]{2,1,0:T(4,128)} %x_hbm.1, s32[1,128]{1,0:T(1,128)} %cell_ref.1, f32[1,128]{1,0:T(1,128)} %value_ref.1, f32[1,128]{1,0:T(1,128)} %var_ref.1, s32[1,2]{1,0:T(1,128)} %rows_ref.1), custom_call_target="tpu_custom_call" | custom-call | tf_op jit(solution)/shard_map/engine/pallas_call | solution.py:650
  57.4 2.2 %settle.1 = f32[160,4,256]{2,1,0:T(4,128)} custom-call(f32[32,5,8,128]{3,2,1,0:T(8,128)} %engine.1.z_hbm), custom_call_target="tpu_custom_call" | custom-call | tf_op jit(solution)/shard_map/settle/pallas_call | solution.py:713

commit v6 on v5

--- a/solution.py
+++ b/solution.py
@@ -258,18 +258,33 @@
     ]
 
 
-def products(work, y, at):
+def own_products(work, y, right):
     common, crossed, y_right, y_turned = work[:4]
-    near = y.shape[0]
-    put_right(y_right, 0, y)
-    yh, yl = y_right[0:near], y_right[near : 2 * near]
-    ah, al = split(at)
-    y_turned[...] = yh.T
-    right = jnp.concatenate([yh, ah], axis=0)
-    right = jnp.concatenate([right, jnp.concatenate([yl, al], axis=0), right], axis=1)
-    both = dot_across(jnp.concatenate([yh, yh, yl], axis=1), right)
-    common[...] = both[:, :near]
-    crossed[...] = both[:, near:]
+    side = y.shape[0]
+    put_right(y_right, side, y)
+    high, low = y_right[side : 2 * side], y_right[4 * side : 5 * side]
+    left = jnp.concatenate([high, high, low], axis=1)
+    crossed[side : 2 * side] = dot_across(left, right)
+    common[side : 2 * side, side : 2 * side] = dot_across(left, jnp.concatenate([high, low, high], axis=1))
+
+
+def other_products(work, sides, right):
+    common, crossed, y_right, y_turned = work[:4]
+    side = sides[0].shape[0]
+    for slot, y in zip((0, 2), sides):
+        put_right(y_right, slot * side, y)
+    near = 3 * side
+    high, low = y_right[0:near], y_right[near : 2 * near]
+    y_turned[...] = high.T
+    terms = [jnp.concatenate([v[0:side], v[2 * side :]], axis=0) for v in (high, low)]
+    left = jnp.concatenate([terms[0], terms[0], terms[1]], axis=1)
+    mine = dot_across(left, jnp.concatenate([high, low, high], axis=1))
+    apart = dot_across(left, right)
+    for i, slot in enumerate((0, 2)):
+        span = slice(slot * side, (slot + 1) * side)
+        common[span] = mine[i * side : (i + 1) * side]
+        crossed[span] = apart[i * side : (i + 1) * side]
+        common[side : 2 * side, span] = mine[i * side : (i + 1) * side, side : 2 * side].T
 
 
 def solve_patch(dims, work, slot, spare_first, lower, upper, innov, meta):
@@ -318,10 +333,9 @@
         x_left[i : i + tile] = left_form(x)
         put_right(x_right, i, x)
         keep(i, block, jnp.where(lane == spare, innov[i : i + tile], crossed[i : i + tile]) * scale_col[i : i + tile])
-    for i in tiles:
-        x2 = dot(x_left[i : i + tile], x_right[...])
-        x3 = dot(left_form(x2), x_right[...])
-        low_left[i : i + tile] = left_form(c2 * x_tile(i) + c3 * x2 + c4 * x3)
+    x2 = dot(x_left[...], x_right[...])
+    x3 = dot(left_form(x2), x_right[...])
+    low_left[...] = left_form(c2 * (common[...] * scale_col * scale_row) + c3 * x2 + c4 * x3)
 
     def low_on(i, which):
         return dot(low_left[i : i + tile], b_right[which])
@@ -431,9 +445,9 @@
     reads = [
         pltpu.make_async_copy(x_hbm.at[pl.ds(kc * group, group)], x_buf.at[kc], x_sem.at[kc]) for kc in range(chunks)
     ]
+    barrier, partners = greet_all(lats, members)
     for read in reads:
         read.start()
-    barrier, partners = greet_all(lats, members)
 
     obs_out[...] = jnp.zeros_like(obs_out)
     obs_out[0:1, :] = cell_ref[...].astype(jnp.float32)
@@ -540,15 +554,23 @@
     mean = jnp.sum(states, axis=1, keepdims=True) * (1.0 / states.shape[1])
     at = states - mean
     at_buf[...] = at
+    ah, al = split(at)
+    right = jnp.concatenate([ah, al, ah], axis=1)
+
+    def observed(slot):
+        raw = jnp.concatenate([yt[slot, kc] for kc in range(chunks)], axis=1)
+        centre = jnp.sum(raw, axis=1, keepdims=True) * (1.0 / raw.shape[1])
+        return raw - centre, centre
+
+    own_spread, own_mean = observed(1)
+    own_products(work, own_spread, right)
     for copy in late:
         copy.wait_recv()
-    y_raw = jnp.concatenate(
-        [jnp.concatenate([yt[slot, kc] for kc in range(chunks)], axis=1) for slot in range(3)], axis=0
-    )
-    y_mean = jnp.sum(y_raw, axis=1, keepdims=True) * (1.0 / y_raw.shape[1])
+    before, before_mean = observed(0)
+    after, after_mean = observed(2)
+    other_products(work, (before, after), right)
     all_meta = jnp.concatenate([meta[slot] for slot in range(3)], axis=1)
-    innov = to_column(all_meta[0:1]) - y_mean
-    products(work, y_raw - y_mean, at)
+    innov = to_column(all_meta[0:1]) - jnp.concatenate([before_mean, own_mean, after_mean], axis=0)
     y_right, turned = work[2], work[9]
 
     nobs = cell_lane.shape[1]

time: 60.5 us -> 60 us (level)
  no operation moved by 1% of the time
where the time goes in v6:
time: 60 us; the launch traced here: 59.3 us
  Pallas kernels  59.1 us (98%)
    pallas_call x1, Pallas kernels, engine(): pl.pallas_call(functools.partial(engine_kernel, dims), out_shape=jax.Shap...  56.9 us
    pallas_call x1, Pallas kernels, settle(): pl.pallas_call(functools.partial(settle_kernel, dims), out_shape=jax.Shap...  2.2 us

profile of v6, /device:TPU:11, one launch (start us, length us, event | category | flops | bytes accessed | tf_op | source)
XLA Modules:
  0.0 59.3 jit_solution(16909464721303832866)
XLA Ops:
  0.0 56.9 %engine.1.z_hbm = f32[32,5,8,128]{3,2,1,0:T(8,128)} custom-call(f32[160,4,256]{2,1,0:T(4,128)} %x_hbm.1, s32[1,128]{1,0:T(1,128)} %cell_ref.1, f32[1,128]{1,0:T(1,128)} %value_ref.1, f32[1,128]{1,0:T(1,128)} %var_ref.1, s32[1,2]{1,0:T(1,128)} %rows_ref.1), custom_call_target="tpu_custom_call" | custom-call | tf_op jit(solution)/shard_map/engine/pallas_call | solution.py:672
  56.9 2.2 %settle.1 = f32[160,4,256]{2,1,0:T(4,128)} custom-call(f32[32,5,8,128]{3,2,1,0:T(8,128)} %engine.1.z_hbm), custom_call_target="tpu_custom_call" | custom-call | tf_op jit(solution)/shard_map/settle/pallas_call | solution.py:735

commit v7 on v6

--- a/solution.py
+++ b/solution.py
@@ -287,13 +287,7 @@
         common[side : 2 * side, span] = mine[i * side : (i + 1) * side, side : 2 * side].T
 
 
-def solve_patch(dims, work, slot, spare_first, lower, upper, innov, meta):
-    lats, members, chunks, rows, width, group = dims
-    common, crossed, y_right, y_turned, x_left, x_right, low_left, b_right, blocks, turned = work
-    count, near = y_turned.shape
-    cells = crossed.shape[1]
-    tile = near // 2
-    tiles = range(0, near, tile)
+def weigh(width, cells, near, lower, upper, meta):
     var, obs_rows = meta[1:2], meta[2:3]
     strip_of = lax.broadcasted_iota(jnp.int32, (1, near), 1) // (near // 3) - 1
     cols = meta[3:4] + (strip_of * width).astype(jnp.float32)
@@ -301,7 +295,17 @@
     lat_gap = jnp.maximum(jnp.maximum(lower - obs_rows, obs_rows - upper), 0.0) / (cells // width / 4.0)
     weights = jnp.exp(-lat_gap * lat_gap - lon_gap * lon_gap) / var
     scale = jnp.sqrt(weights)
-    scale_col = to_column(scale)
+    return weights, scale, to_column(scale)
+
+
+def solve_patch(dims, work, slot, spare_first, near_weights, innov):
+    lats, members, chunks, rows, width, group = dims
+    common, crossed, y_right, y_turned, x_left, x_right, low_left, b_right, blocks, turned = work
+    count, near = y_turned.shape
+    cells = crossed.shape[1]
+    tile = near // 2
+    tiles = range(0, near, tile)
+    weights, scale, scale_col = near_weights
 
     left = (y_turned[...].astype(jnp.float32) * weights).astype(jnp.bfloat16)
     gram = jnp.abs(dot(left, y_right[0:near]))
@@ -562,17 +566,9 @@
         centre = jnp.sum(raw, axis=1, keepdims=True) * (1.0 / raw.shape[1])
         return raw - centre, centre
 
-    own_spread, own_mean = observed(1)
-    own_products(work, own_spread, right)
-    for copy in late:
+    for copy in late[:2]:
         copy.wait_recv()
-    before, before_mean = observed(0)
-    after, after_mean = observed(2)
-    other_products(work, (before, after), right)
     all_meta = jnp.concatenate([meta[slot] for slot in range(3)], axis=1)
-    innov = to_column(all_meta[0:1]) - jnp.concatenate([before_mean, own_mean, after_mean], axis=0)
-    y_right, turned = work[2], work[9]
-
     nobs = cell_lane.shape[1]
     sure = lats // 4
     rest = lats - sure
@@ -584,6 +580,16 @@
     for which in (lasts, 1.0 - lasts):
         lower = which * first_len
         spans.append((lower, lower + (first_len + which * (second_len - first_len)) - 1.0))
+    near_weights = [weigh(width, cells, 3 * nobs, *span, all_meta) for span in spans]
+    own_spread, own_mean = observed(1)
+    own_products(work, own_spread, right)
+    for copy in late[2:]:
+        copy.wait_recv()
+    before, before_mean = observed(0)
+    after, after_mean = observed(2)
+    other_products(work, (before, after), right)
+    innov = to_column(all_meta[0:1]) - jnp.concatenate([before_mean, own_mean, after_mean], axis=0)
+    y_right, turned = work[2], work[9]
 
     def finish(tile, tiles, pick_cells, weights, change, factor):
         begin = tile * (rows * width)
@@ -609,7 +615,7 @@
     z_copies = []
     cut, tail = sure * rows * width, rest * rows * width
     early = last * rest
-    change, factor = solve_patch(dims, work, 0, last, *spans[0], innov, all_meta)
+    change, factor = solve_patch(dims, work, 0, last, near_weights[0], innov)
     change_col = to_column(change)
 
     def far(column):
@@ -623,7 +629,7 @@
         for dm in range(members):
             give(((m + dm) % members, early + l))
 
-    change2, factor2 = solve_patch(dims, work, 1, 1 - last, *spans[1], innov, all_meta)
+    change2, factor2 = solve_patch(dims, work, 1, 1 - last, near_weights[1], innov)
     cell_row = (lax.broadcasted_iota(jnp.int32, (cells, 1), 0) // width).astype(jnp.float32)
     inside = near(jnp.logical_and(cell_row >= spans[0][0], cell_row <= spans[0][1]).astype(jnp.float32)) > 0.5
     base = (1 - last) * sure

time: 60 us -> 60 us (level)
  no operation moved by 1% of the time
where the time goes in v7:
time: 60 us; the launch traced here: 59.3 us
  Pallas kernels  59.2 us (99%)
    pallas_call x1, Pallas kernels, engine(): pl.pallas_call(functools.partial(engine_kernel, dims), out_shape=jax.Shap...  57 us
    pallas_call x1, Pallas kernels, settle(): pl.pallas_call(functools.partial(settle_kernel, dims), out_shape=jax.Shap...  2.2 us

profile of v7, /device:TPU:11, one launch (start us, length us, event | category | flops | bytes accessed | tf_op | source)
XLA Modules:
  0.0 59.3 jit_solution(6777047584333029619)
XLA Ops:
  0.0 57.0 %engine.1.z_hbm = f32[32,5,8,128]{3,2,1,0:T(8,128)} custom-call(f32[160,4,256]{2,1,0:T(4,128)} %x_hbm.1, s32[1,128]{1,0:T(1,128)} %cell_ref.1, f32[1,128]{1,0:T(1,128)} %value_ref.1, f32[1,128]{1,0:T(1,128)} %var_ref.1, s32[1,2]{1,0:T(1,128)} %rows_ref.1), custom_call_target="tpu_custom_call" | custom-call | tf_op jit(solution)/shard_map/engine/pallas_call | solution.py:678
  57.0 2.2 %settle.1 = f32[160,4,256]{2,1,0:T(4,128)} custom-call(f32[32,5,8,128]{3,2,1,0:T(8,128)} %engine.1.z_hbm), custom_call_target="tpu_custom_call" | custom-call | tf_op jit(solution)/shard_map/settle/pallas_call | solution.py:741
